TPU v7x, 512 devices: a 8x2x16 block of a 8x8x16 slice. The times are simulated.
512 devices in a mesh: groups: 2 (over y), expert: 32 (over z, core), hidden: 8 (over x).
Axes of the slice: x: 8, y: 2, z: 16, core: 2. Of those that a mesh axis runs over, the one named last changes fastest.
The devices are a block of a 8x8x16 slice.
Arguments:
- tokens: bfloat16 [4096, 4096], P(('groups', 'expert'), 'hidden'), parts along dimension 0, may hold values from -6 to 6
- norm_gain: bfloat16 [4096], P('hidden'), may hold values from 0.25 to 1.75
- gate_proj: bfloat16 [64, 768, 4096], P('expert', 'hidden'), may hold values from -0.09375 to 0.09375
- up_proj: bfloat16 [64, 768, 4096], P('expert', 'hidden'), may hold values from -0.09375 to 0.09375
- down_proj: bfloat16 [64, 768, 4096], P('expert', 'hidden'), may hold values from -0.21875 to 0.21875
- expert_ids: int32 [4096, 8], P(('groups', 'expert')), parts along dimension 0, may hold values from 0 to 63, as said below
- slot_ids: int32 [4096, 8], P(('groups', 'expert')), parts along dimension 0, may hold values from 0 to 11, as said below
- gate_num: int32 [4096, 8], P(('groups', 'expert')), parts along dimension 0, may hold values from 1 to 255
Outputs:
- layer_out: bfloat16 [4096, 4096], P(('groups', 'expert'), 'hidden'), parts along dimension 0
There are 2 independent parts, one for each index of `groups`. A program takes and returns all parts, laid end to end along the dimension named above; an argument that names none is the same for every part. Nothing has to cross between parts.
Inputs may be any that keep to these rules, and one draw needn't show every extreme that they name: `expert_ids`: each token names 8 different experts. In every aligned block of 64 tokens (the tokens of one index of the expert axis), a quarter of the experts are named by exactly 12 tokens, a quarter by 8 and the other half by 6; some expert is named by 12 tokens in every block. `slot_ids`: within an aligned block of 64 tokens, the routes that name one expert carry the slots 0 up to their count minus 1, each once.
All inputs are finite; a program needn't handle non-finite values.
Results may differ from a plain program's by a relative error of at most 0.0085.
Values may be sent and summed in bfloat16 or wider, within the bound.
No kernel may reach another device: no remote copies, remote signals or barrier semaphores. Data moves between devices by JAX's collectives and lax.ppermute only.
A program may use at most 64 MiB of HBM per device.

v0:
```python
import jax
import jax.numpy as jnp
from jax import lax
from jax.experimental import pallas as pl
from jax.experimental.pallas import tpu as pltpu
from jax.sharding import Mesh
from jax.sharding import PartitionSpec as P

CAP = 12
HALVES = 2
LIMIT = 20 * 2**20
EXPERT = ("expert_0", "expert_1")
GROUPS_EXPERT = ("groups", "expert_0", "expert_1")


gate_scale = 1.0 / 1024.0


def shifted(array, step):
    devices = lax.axis_size("hidden")
    return lax.ppermute(array, "hidden", [(i, (i + step) % devices) for i in range(devices)])


def feature_block(weights, index, width):
    return lax.dynamic_slice_in_dim(weights, index * width, width, axis=weights.ndim - 1)


def sent(tiles, axes):
    return lax.all_to_all(tiles, axes, split_axis=0, concat_axis=0, tiled=True)


def in_two_stages(tiles):
    shape = [lax.axis_size(a) for a in EXPERT]
    tiles = tiles.reshape(*shape, *tiles.shape[1:])
    for k in (1, 0):
        tiles = lax.all_to_all(tiles, EXPERT[k], split_axis=k, concat_axis=k, tiled=True)
    return tiles


def route_tables(expert_ids, slot_ids, gate_num, slots):
    slot_index = expert_ids * CAP + slot_ids
    columns = lax.broadcasted_iota(jnp.int32, (1, 1, slots), 2)
    matches = slot_index[:, :, None] == columns
    placing = jnp.any(matches, axis=1).astype(jnp.bfloat16)
    scaled = gate_num.astype(jnp.float32) * gate_scale
    weights = jnp.sum(jnp.where(matches, scaled[:, :, None], 0.0), axis=1).astype(jnp.bfloat16)
    return (placing, weights)


def unpacked(turns, pieces, parts, rows, width):
    arrays = []
    for _, array, *_ in pieces:
        if not any(array is known for known in arrays):
            arrays.append(array)

    def place(array):
        return [array is known for known in arrays].index(True)

    def body(turn, *refs):
        sources, (down, gains, sems) = refs[: len(arrays)], refs[len(arrays) :]
        moves = []
        for n, (d, array, low, at, count) in enumerate(pieces):
            target = gains.at[d] if at is None else down.at[turn[d], pl.ds(at, count)]
            source = sources[place(array)].at[pl.ds(low, count)]
            moves.append(pltpu.make_async_copy(source, target, sems.at[n]))
        for move in moves:
            move.start()
        for move in moves:
            move.wait()

    vmem = pl.BlockSpec(memory_space=pltpu.VMEM)
    return pl.pallas_call(
        body,
        out_shape=[
            jax.ShapeDtypeStruct((parts, rows, width), jnp.bfloat16),
            jax.ShapeDtypeStruct((parts, 8, width), jnp.bfloat16),
        ],
        in_specs=[pl.BlockSpec(memory_space=pltpu.SMEM)]
        + [pl.BlockSpec(memory_space=pltpu.HBM)] * len(arrays),
        out_specs=[vmem] * 2,
        scratch_shapes=[pltpu.SemaphoreType.DMA((len(pieces),))],
        compiler_params=pltpu.CompilerParams(vmem_limit_bytes=LIMIT),
        cost_estimate=pl.CostEstimate(
            flops=10**8, bytes_accessed=4 * parts * rows * width, transcendentals=0
        ),
    )(turns, *arrays)


def add_blocks(turns, gate_proj, up_proj, gains, blocks, before, finish):
    local, units, features = gate_proj.shape
    parts, _, width = gains.shape
    count = len(blocks)
    pieces = [piece for group in blocks.values() for piece in group]
    rows_all = sum(piece.shape[0] for piece in pieces) // count
    wide = 2 * local * units
    shapes = [
        jax.ShapeDtypeStruct((wide, rows_all), jnp.float32),
        jax.ShapeDtypeStruct((rows_all, 128), jnp.float32),
    ]

    def body(turn, gate, up, gain_ref, *refs):
        block_refs, refs = list(refs[: len(pieces)]), refs[len(pieces) :]
        start_sums, start_squares = refs[:2] if before else (None, None)
        refs = refs[2:] if before else refs
        out, (sums, squares) = (refs[0], refs[1:]) if finish else (None, refs)
        for n, (d, group) in enumerate(blocks.items()):
            start = pl.multiple_of(turn[d] * width, 128)
            cut = jnp.concatenate(
                [w[e, :, pl.ds(start, width)] for w in (gate, up) for e in range(local)], axis=0
            )
            cut = cut * gain_ref[d, 0:1, :]
            first = 0
            for piece in group:
                rows = block_refs.pop(0)[...]
                here = pl.ds(first, piece.shape[0])
                first += piece.shape[0]
                product = lax.dot_general(
                    cut, rows, (((1,), (1,)), ((), ())), preferred_element_type=jnp.float32
                )
                square = jnp.square(rows.astype(jnp.float32))
                square = sum(square[:, k : k + 128] for k in range(0, width, 128))
                if n or before:
                    old_sums, old_squares = (sums, squares) if n else (start_sums, start_squares)
                    product = product + old_sums[:, here]
                    square = square + old_squares[here, :]
                sums[:, here] = product
                squares[here, :] = square
        if finish:
            total = jnp.sum(squares[...].T, axis=0, keepdims=True)
            scale = lax.rsqrt(total / features + 0.5)
            owner = lax.broadcasted_iota(jnp.int32, (1, rows_all), 1) % (local * CAP) // CAP
            own = []
            for k in range(2):
                value = sums[pl.ds(k * local * units, units), :]
                for e in range(1, local):
                    other = sums[pl.ds((k * local + e) * units, units), :]
                    value = jnp.where(owner == e, other, value)
                own.append(value * scale)
            done = (own[0] / (1.0 + jnp.exp(-own[0])) * own[1]).astype(jnp.bfloat16)
            for j in range(parts):
                out[j] = done

    vmem = pl.BlockSpec(memory_space=pltpu.VMEM)
    held = [] if before is None else list(before)
    done = jax.ShapeDtypeStruct((parts, units, rows_all), jnp.bfloat16)
    return pl.pallas_call(
        body,
        out_shape=done if finish else shapes,
        in_specs=[pl.BlockSpec(memory_space=pltpu.SMEM)] + [vmem] * (3 + len(pieces) + len(held)),
        out_specs=vmem if finish else [vmem] * 2,
        scratch_shapes=[pltpu.VMEM(s.shape, s.dtype) for s in shapes] if finish else [],
        compiler_params=pltpu.CompilerParams(vmem_limit_bytes=LIMIT),
        cost_estimate=pl.CostEstimate(
            flops=2 * wide * width * rows_all * count, bytes_accessed=0, transcendentals=0
        ),
    )(turns, gate_proj, up_proj, gains, *pieces, *held)


def layer(tokens, norm_gain, gate_proj, up_proj, down_proj, expert_ids, slot_ids, gate_num):
    parts = lax.axis_size("hidden")
    here = lax.axis_index("hidden")
    sources = lax.axis_size(EXPERT)
    local, units, _ = gate_proj.shape
    width = tokens.shape[1]
    per_source = local * CAP
    rows_all = sources * per_source
    down_rows = local * units

    full = (parts - 1) // 2
    order = [0]
    for s in range(1, full + 1):
        order += [s, parts - s]
    order.append(full + 1)

    gain_rows = jnp.broadcast_to(norm_gain[None, :], (8, width))
    cuts = [
        feature_block(down_proj, (here + d) % parts, width).reshape(down_rows, width)
        for d in range(parts)
    ]
    far = full + 1
    kept = down_rows - units
    cut_by_shift = [jnp.concatenate([cut, gain_rows], axis=0) for cut in cuts]
    cut_by_shift[far] = jnp.concatenate([cuts[far][:kept], gain_rows], axis=0)
    one, three = parts - 1, parts - (far - 1)
    end = down_rows + 8
    first = shifted(jnp.concatenate([cut_by_shift[one], cuts[far][kept:]], axis=0), one)
    for d in range(1, parts):
        if d not in (one, three):
            cut_by_shift[d] = shifted(cut_by_shift[d], d)
    cut_by_shift[one] = first
    cut_by_shift[three] = shifted(
        jnp.concatenate([cut_by_shift[three], first[end:]], axis=0), three
    )
    turns = jnp.stack([(here - d + parts) % parts for d in range(parts)]).astype(jnp.int32)
    pieces = []
    for d, cut in enumerate(cut_by_shift):
        pieces.append((d, cut, 0, 0, kept if d == far else down_rows))
        pieces.append((d, cut, kept if d == far else down_rows, None, 8))
    pieces.append((far, cut_by_shift[three], end, kept, units))
    down_all, gains = unpacked(turns, pieces, parts, down_rows, width)

    placing, weights = route_tables(expert_ids, slot_ids, gate_num, rows_all)
    outgoing = lax.dot_general(
        placing, tokens, (((0,), (0,)), ((), ())), preferred_element_type=jnp.float32
    ).astype(jnp.bfloat16)
    received = in_two_stages(outgoing.reshape(sources, per_source, width))
    received = received.reshape(rows_all, width)

    size = rows_all // HALVES
    owner = (lax.broadcasted_iota(jnp.int32, (1, rows_all), 1) % per_source) // CAP
    halves = [received[k * size : (k + 1) * size] for k in range(HALVES)]
    blocks = [{0: half} for half in halves]
    ahead, back = list(halves), list(halves)
    for s in range(1, full + 1):
        for k in range(HALVES):
            ahead[k] = blocks[k][s] = shifted(ahead[k], 1)
            back[k] = blocks[k][parts - s] = shifted(back[k], -1)
    early = [d for d in order if min(d, parts - d) < full]
    held = add_blocks(
        turns, gate_proj, up_proj, gains, {d: [b[d] for b in blocks] for d in early}, None, False
    )
    ahead[0], back[1], held = lax.optimization_barrier((ahead[0], back[1], held))
    blocks[0][far] = shifted(ahead[0], 1)
    blocks[1][far] = shifted(back[1], -1)
    late = [d for d in order if d not in early]
    copies = add_blocks(
        turns, gate_proj, up_proj, gains, {d: [b[d] for b in blocks] for d in late}, held, True
    )
    held = (copies, down_all, weights, owner)
    copies, down_all, weights, owner = lax.optimization_barrier(held)
    gathered = sent(copies, "hidden")
    gathered = gathered.reshape(parts * units, rows_all)
    result = jnp.zeros((rows_all, width), jnp.float32)
    for e in range(local):
        spread = jnp.where(owner == e, gathered, jnp.zeros_like(gathered))
        down = down_all[:, e * units : (e + 1) * units].reshape(parts * units, width)
        result = result + lax.dot_general(
            spread, down, (((0,), (0,)), ((), ())), preferred_element_type=jnp.float32
        )

    tiles = result.astype(jnp.bfloat16).reshape(sources, per_source, width)
    returned = sent(tiles, EXPERT).reshape(rows_all, width)
    combined = jnp.dot(weights, returned, preferred_element_type=jnp.float32)
    return combined.astype(jnp.bfloat16)


def solution(mesh):
    torus = Mesh(
        mesh.devices.reshape(
            mesh.shape["groups"], mesh.shape["expert"] // 2, 2, mesh.shape["hidden"]
        ),
        ("groups", "expert_0", "expert_1", "hidden"),
    )
    in_specs = (
        P(GROUPS_EXPERT, "hidden"),
        P("hidden"),
        P(EXPERT, "hidden", None),
        P(EXPERT, "hidden", None),
        P(EXPERT, "hidden", None),
        P(GROUPS_EXPERT, None),
        P(GROUPS_EXPERT, None),
        P(GROUPS_EXPERT, None),
    )
    out_specs = P(GROUPS_EXPERT, "hidden")
    return jax.shard_map(layer, mesh=torus, in_specs=in_specs, out_specs=out_specs, check_vma=False)
```

profile of v0, /device:TPU:65, one launch (start us, length us, event | category | flops | bytes accessed | tf_op | source)
XLA Modules:
  0.0 319.0 jit_solution(12210208309671819886)
XLA Ops:
  1.9 45.4 %all_to_all.20 = bf16[16,2,24,512]{3,2,0,1:T(8,128)(2,1)S(1)} all-to-all(bf16[16,2,24,512]{3,2,0,1:T(8,128)(2,1)S(1)} %copy.21), channel_id=1, replica_groups=mesh['groups'=2,'expert_0'=16,'expert_1'=2,'hidden'=8] {'expert_1'}, dimensions={1} | all-to-all | bytes 1572864 | tf_op jit(solution)/shard_map/all_to_all | solution.py:36
  48.3 4.1 %all-to-all-start.1 = ((bf16[16,2,24,512]{3,2,1,0:T(8,128)(2,1)}), bf16[16,2,24,512]{3,2,1,0:T(8,128)(2,1)S(1)}, u32[]{:S(2)}, u32[]{:S(2)}) async-start(bf16[16,2,24,512]{3,2,1,0:T(8,128)(2,1)} %copy.22), calls=%async_computation.1 | async-start | bytes 1572864 | tf_op jit(solution)/shard_map/all_to_all | solution.py:36
  57.0 4.3 %collective-permute-start.1 = (bf16[200,512]{1,0:T(8,128)(2,1)}, bf16[200,512]{1,0:T(8,128)(2,1)S(1)}, u32[]{:S(2)}, u32[]{:S(2)}) collective-permute-start(bf16[200,512]{1,0:T(8,128)(2,1)} %get-tuple-element.44), channel_id=1, source_target_pairs={{0,2},{1,3},{2,4},{3,5},{4,6},{5,7},{6,0},{7,1},{8,10},{9,11},{10,... | collective-permute-start | bytes 614408 | tf_op jit(solution)/shard_map/ppermute | solution.py:21
  61.4 5.0 %collective-permute-start.3 = (bf16[104,512]{1,0:T(8,128)(2,1)S(1)}, bf16[104,512]{1,0:T(8,128)(2,1)S(1)}, u32[]{:S(2)}, u32[]{:S(2)}) collective-permute-start(bf16[104,512]{1,0:T(8,128)(2,1)S(1)} %pad_maximum_fusion.7), channel_id=1, source_target_pairs={{0,4},{1,5},{2,6},{3,7},{4,0},{5,1},{6,2},{7,3},{8,12},{9,13},{10,... | collective-permute-start | bytes 319496 | tf_op jit(solution)/shard_map/ppermute | solution.py:21
  66.4 20.1 %all-to-all-done.1 = bf16[16,2,24,512]{3,2,1,0:T(8,128)(2,1)S(1)} async-done(((bf16[16,2,24,512]{3,2,1,0:T(8,128)(2,1)}), bf16[16,2,24,512]{3,2,1,0:T(8,128)(2,1)S(1)}, u32[]{:S(2)}, u32[]{:S(2)}) %all-to-all-start.1) | async-done | bytes 786464 | tf_op jit(solution)/shard_map/all_to_all | solution.py:36
  86.6 4.8 %collective-permute-start.16 = (bf16[384,512]{1,0:T(8,128)(2,1)S(1)}, bf16[384,512]{1,0:T(8,128)(2,1)S(1)}, u32[]{:S(2)}, u32[]{:S(2)}) collective-permute-start(bf16[384,512]{1,0:T(8,128)(2,1)S(1)} %bitcast.34), channel_id=1, source_target_pairs={{0,7},{1,0},{2,1},{3,2},{4,3},{5,4},{6,5},{7,6},{8,15},{9,8},{10,9... | collective-permute-start | bytes 1179656 | tf_op jit(solution)/shard_map/ppermute | solution.py:21
  94.0 4.5 %collective-permute-start.2 = (bf16[200,512]{1,0:T(8,128)(2,1)}, bf16[200,512]{1,0:T(8,128)(2,1)S(1)}, u32[]{:S(2)}, u32[]{:S(2)}) collective-permute-start(bf16[200,512]{1,0:T(8,128)(2,1)} %get-tuple-element.45), channel_id=1, source_target_pairs={{0,3},{1,4},{2,5},{3,6},{4,7},{5,0},{6,1},{7,2},{8,11},{9,12},{10,... | collective-permute-start | bytes 614408 | tf_op jit(solution)/shard_map/ppermute | solution.py:21
  99.3 3.3 %collective-permute-start.10 = (bf16[384,512]{1,0:T(8,128)(2,1)S(1)}, bf16[384,512]{1,0:T(8,128)(2,1)}, u32[]{:S(2)}, u32[]{:S(2)}) collective-permute-start(bf16[384,512]{1,0:T(8,128)(2,1)S(1)} %bitcast.35), channel_id=1, source_target_pairs={{0,1},{1,2},{2,3},{3,4},{4,5},{5,6},{6,7},{7,0},{8,9},{9,10},{10,1... | collective-permute-start | bytes 1179656 | tf_op jit(solution)/shard_map/ppermute | solution.py:21
  104.0 3.3 %collective-permute-start.13 = (bf16[384,512]{1,0:T(8,128)(2,1)S(1)}, bf16[384,512]{1,0:T(8,128)(2,1)}, u32[]{:S(2)}, u32[]{:S(2)}) collective-permute-start(bf16[384,512]{1,0:T(8,128)(2,1)S(1)} %bitcast.38), channel_id=1, source_target_pairs={{0,7},{1,0},{2,1},{3,2},{4,3},{5,4},{6,5},{7,6},{8,15},{9,8},{10,9... | collective-permute-start | bytes 1179656 | tf_op jit(solution)/shard_map/ppermute | solution.py:21
  115.4 3.4 %collective-permute-start.8 = (bf16[384,512]{1,0:T(8,128)(2,1)S(1)}, bf16[384,512]{1,0:T(8,128)(2,1)}, u32[]{:S(2)}, u32[]{:S(2)}) collective-permute-start(bf16[384,512]{1,0:T(8,128)(2,1)S(1)} %collective-permute-done.7.refs_2_), channel_id=1, source_target_pairs={{0,1},{1,2},{2,3},{3,4},{4,5},{5,6},{6,7},{7,0},{8,9},{9,10},{10,1... | collective-permute-start | bytes 1179656 | tf_op jit(solution)/shard_map/ppermute | solution.py:21
  119.5 5.4 %collective-permute-start.6 = (bf16[200,512]{1,0:T(8,128)(2,1)S(1)}, bf16[200,512]{1,0:T(8,128)(2,1)S(1)}, u32[]{:S(2)}, u32[]{:S(2)}) collective-permute-start(bf16[200,512]{1,0:T(8,128)(2,1)S(1)} %copy-done.31), channel_id=1, source_target_pairs={{0,6},{1,7},{2,0},{3,1},{4,2},{5,3},{6,4},{7,5},{8,14},{9,15},{10,... | collective-permute-start | bytes 614408 | tf_op jit(solution)/shard_map/ppermute | solution.py:21
  127.7 4.6 %collective-permute-start.14 = (bf16[384,512]{1,0:T(8,128)(2,1)}, bf16[384,512]{1,0:T(8,128)(2,1)}, u32[]{:S(2)}, u32[]{:S(2)}) collective-permute-start(bf16[384,512]{1,0:T(8,128)(2,1)} %collective-permute-done.13.refs_4_), channel_id=1, source_target_pairs={{0,7},{1,0},{2,1},{3,2},{4,3},{5,4},{6,5},{7,6},{8,15},{9,8},{10,9... | collective-permute-start | bytes 1179656 | tf_op jit(solution)/shard_map/ppermute | solution.py:21
  134.6 3.8 %collective-permute-start.5 = (bf16[296,512]{1,0:T(8,128)(2,1)}, bf16[296,512]{1,0:T(8,128)(2,1)}, u32[]{:S(2)}, u32[]{:S(2)}) collective-permute-start(bf16[296,512]{1,0:T(8,128)(2,1)} %fusion.11), channel_id=1, source_target_pairs={{0,5},{1,6},{2,7},{3,0},{4,1},{5,2},{6,3},{7,4},{8,13},{9,14},{10,... | collective-permute-start | bytes 909320 | tf_op jit(solution)/shard_map/ppermute | solution.py:21
  138.5 4.4 %collective-permute-start.18 = (bf16[384,512]{1,0:T(8,128)(2,1)}, bf16[384,512]{1,0:T(8,128)(2,1)}, u32[]{:S(2)}, u32[]{:S(2)}) collective-permute-start(bf16[384,512]{1,0:T(8,128)(2,1)} %collective-permute-done.17.refs_9_), channel_id=1, source_target_pairs={{0,7},{1,0},{2,1},{3,2},{4,3},{5,4},{6,5},{7,6},{8,15},{9,8},{10,9... | collective-permute-start | bytes 1179656 | tf_op jit(solution)/shard_map/ppermute | solution.py:21
  144.9 13.2 %collective-permute-done.5.refs_5_ = bf16[296,512]{1,0:T(8,128)(2,1)} collective-permute-done((bf16[296,512]{1,0:T(8,128)(2,1)}, bf16[296,512]{1,0:T(8,128)(2,1)}, u32[]{:S(2)}, u32[]{:S(2)}) %collective-permute-start.5) | collective-permute-done | bytes 303136 | tf_op jit(solution)/shard_map/ppermute | solution.py:21
  163.7 3.4 %shard_map.82 = (bf16[8,192,512]{2,1,0:T(8,128)(2,1)S(1)}, bf16[8,8,512]{2,1,0:T(8,128)(2,1)S(1)}) custom-call(s32[8]{0:T(128)S(1)} %stack.35.turn, bf16[200,512]{1,0:T(8,128)(2,1)S(1)} %get-tuple-element.46.refs_0_, bf16[200,512]{1,0:T(8,128)(2,1)S(1)} %copy-done.19, bf16[200,512]{1,0:T(8,128)(2,1)S(1)} %copy-done.21, bf16[200,512]{1,0:T(8,128)(2,1)S(1)} %copy-done.23, ...), custom_call_target="tpu_custom_call" | custom-call | flops 100000000 | bytes 3145728 | tf_op jit(solution)/shard_map/pallas_call | solution.py:72
  168.3 5.2 %collective-permute-start.12 = (bf16[384,512]{1,0:T(8,128)(2,1)}, bf16[384,512]{1,0:T(8,128)(2,1)}, u32[]{:S(2)}, u32[]{:S(2)}) collective-permute-start(bf16[384,512]{1,0:T(8,128)(2,1)} %collective-permute-done.11.refs_7_), channel_id=1, source_target_pairs={{0,1},{1,2},{2,3},{3,4},{4,5},{5,6},{6,7},{7,0},{8,9},{9,10},{10,1... | collective-permute-start | bytes 1179656 | tf_op jit(solution)/shard_map/ppermute | solution.py:21
  179.5 3.8 %shard_map.83 = (f32[384,768]{1,0:T(8,128)S(1)}, f32[768,128]{1,0:T(8,128)S(1)}) custom-call(s32[8]{0:T(128)S(1)} %stack.35.turn, bf16[2,96,4096]{2,1,0:T(8,128)(2,1)S(1)} %copy-done.1, bf16[2,96,4096]{2,1,0:T(8,128)(2,1)S(1)} %copy-done.2, bf16[8,8,512]{2,1,0:T(8,128)(2,1)S(1)} %get-tuple-element.17.gain_ref, bf16[384,512]{1,0:T(8,128)(2,1)S(1)} %bitcast.39, ...), custom_call_target="tpu_custom_call" | custom-call | flops 1509949440 | tf_op jit(solution)/shard_map/pallas_call | solution.py:146
  185.1 3.4 %collective-permute-start.19 = (bf16[384,512]{1,0:T(8,128)(2,1)}, bf16[384,512]{1,0:T(8,128)(2,1)}, u32[]{:S(2)}, u32[]{:S(2)}) collective-permute-start(bf16[384,512]{1,0:T(8,128)(2,1)} %collective-permute-done.9.refs_0_), channel_id=1, source_target_pairs={{0,1},{1,2},{2,3},{3,4},{4,5},{5,6},{6,7},{7,0},{8,9},{9,10},{10,1... | collective-permute-start | bytes 1179656 | tf_op jit(solution)/shard_map/ppermute | solution.py:21
  188.5 3.2 collective-permute-start.20
  192.4 4.7 %collective-permute-done.19.refs_4_ = bf16[384,512]{1,0:T(8,128)(2,1)} collective-permute-done((bf16[384,512]{1,0:T(8,128)(2,1)}, bf16[384,512]{1,0:T(8,128)(2,1)}, u32[]{:S(2)}, u32[]{:S(2)}) %collective-permute-start.19) | collective-permute-done | bytes 393248 | tf_op jit(solution)/shard_map/ppermute | solution.py:21
  205.0 4.2 %all-to-all-start.2 = ((bf16[8,96,768]{2,1,0:T(8,128)(2,1)}), bf16[8,96,768]{2,1,0:T(8,128)(2,1)S(1)}, u32[]{:S(2)}, u32[]{:S(2)}) async-start(bf16[8,96,768]{2,1,0:T(8,128)(2,1)} %copy-done.3), calls=%async_computation.2 | async-start | bytes 2359296 | tf_op jit(solution)/shard_map/all_to_all | solution.py:29
  209.3 19.0 %all-to-all-done.2 = bf16[8,96,768]{2,1,0:T(8,128)(2,1)S(1)} async-done(((bf16[8,96,768]{2,1,0:T(8,128)(2,1)}), bf16[8,96,768]{2,1,0:T(8,128)(2,1)S(1)}, u32[]{:S(2)}, u32[]{:S(2)}) %all-to-all-start.2) | async-done | bytes 1179680 | tf_op jit(solution)/shard_map/all_to_all | solution.py:29
  229.9 88.3 %all_to_all.21 = bf16[32,24,512]{2,1,0:T(8,128)(2,1)S(1)} all-to-all(bf16[32,24,512]{2,1,0:T(8,128)(2,1)S(1)} %bitcast.42), channel_id=1, replica_groups=mesh['groups'=2,'expert_0'=16,'expert_1'=2,'hidden'=8] {'expert_0','expe..., dimensions={0} | all-to-all | bytes 1572864 | tf_op jit(solution)/shard_map/all_to_all | solution.py:29
  (119 shorter events, 53.6 us)
Async XLA Ops:
  48.3 38.2 %all-to-all-start.1 = ((bf16[16,2,24,512]{3,2,1,0:T(8,128)(2,1)}), bf16[16,2,24,512]{3,2,1,0:T(8,128)(2,1)S(1)}, u32[]{:S(2)}, u32[]{:S(2)}) async-start(bf16[16,2,24,512]{3,2,1,0:T(8,128)(2,1)} %copy.22), calls=%async_computation.1 | async-start | bytes 1572864 | tf_op jit(solution)/shard_map/all_to_all | solution.py:36
  54.4 44.2 %collective-permute-start = (bf16[200,512]{1,0:T(8,128)(2,1)}, bf16[200,512]{1,0:T(8,128)(2,1)S(1)}, u32[]{:S(2)}, u32[]{:S(2)}) collective-permute-start(bf16[200,512]{1,0:T(8,128)(2,1)} %get-tuple-element.43), channel_id=1, source_target_pairs={{0,1},{1,2},{2,3},{3,4},{4,5},{5,6},{6,7},{7,0},{8,9},{9,10},{10,1... | collective-permute-start | bytes 614408 | tf_op jit(solution)/shard_map/ppermute | solution.py:21
  57.0 46.3 %collective-permute-start.1 = (bf16[200,512]{1,0:T(8,128)(2,1)}, bf16[200,512]{1,0:T(8,128)(2,1)S(1)}, u32[]{:S(2)}, u32[]{:S(2)}) collective-permute-start(bf16[200,512]{1,0:T(8,128)(2,1)} %get-tuple-element.44), channel_id=1, source_target_pairs={{0,2},{1,3},{2,4},{3,5},{4,6},{5,7},{6,0},{7,1},{8,10},{9,11},{10,... | collective-permute-start | bytes 614408 | tf_op jit(solution)/shard_map/ppermute | solution.py:21
  61.4 32.0 %collective-permute-start.3 = (bf16[104,512]{1,0:T(8,128)(2,1)S(1)}, bf16[104,512]{1,0:T(8,128)(2,1)S(1)}, u32[]{:S(2)}, u32[]{:S(2)}) collective-permute-start(bf16[104,512]{1,0:T(8,128)(2,1)S(1)} %pad_maximum_fusion.7), channel_id=1, source_target_pairs={{0,4},{1,5},{2,6},{3,7},{4,0},{5,1},{6,2},{7,3},{8,12},{9,13},{10,... | collective-permute-start | bytes 319496 | tf_op jit(solution)/shard_map/ppermute | solution.py:21
  86.6 26.1 %collective-permute-start.16 = (bf16[384,512]{1,0:T(8,128)(2,1)S(1)}, bf16[384,512]{1,0:T(8,128)(2,1)S(1)}, u32[]{:S(2)}, u32[]{:S(2)}) collective-permute-start(bf16[384,512]{1,0:T(8,128)(2,1)S(1)} %bitcast.34), channel_id=1, source_target_pairs={{0,7},{1,0},{2,1},{3,2},{4,3},{5,4},{6,5},{7,6},{8,15},{9,8},{10,9... | collective-permute-start | bytes 1179656 | tf_op jit(solution)/shard_map/ppermute | solution.py:21
  91.4 23.9 %collective-permute-start.7 = (bf16[384,512]{1,0:T(8,128)(2,1)S(1)}, bf16[384,512]{1,0:T(8,128)(2,1)S(1)}, u32[]{:S(2)}, u32[]{:S(2)}) collective-permute-start(bf16[384,512]{1,0:T(8,128)(2,1)S(1)} %bitcast.37), channel_id=1, source_target_pairs={{0,1},{1,2},{2,3},{3,4},{4,5},{5,6},{6,7},{7,0},{8,9},{9,10},{10,1... | collective-permute-start | bytes 1179656 | tf_op jit(solution)/shard_map/ppermute | solution.py:21
  94.0 15.1 %collective-permute-start.2 = (bf16[200,512]{1,0:T(8,128)(2,1)}, bf16[200,512]{1,0:T(8,128)(2,1)S(1)}, u32[]{:S(2)}, u32[]{:S(2)}) collective-permute-start(bf16[200,512]{1,0:T(8,128)(2,1)} %get-tuple-element.45), channel_id=1, source_target_pairs={{0,3},{1,4},{2,5},{3,6},{4,7},{5,0},{6,1},{7,2},{8,11},{9,12},{10,... | collective-permute-start | bytes 614408 | tf_op jit(solution)/shard_map/ppermute | solution.py:21
  99.3 26.4 %collective-permute-start.10 = (bf16[384,512]{1,0:T(8,128)(2,1)S(1)}, bf16[384,512]{1,0:T(8,128)(2,1)}, u32[]{:S(2)}, u32[]{:S(2)}) collective-permute-start(bf16[384,512]{1,0:T(8,128)(2,1)S(1)} %bitcast.35), channel_id=1, source_target_pairs={{0,1},{1,2},{2,3},{3,4},{4,5},{5,6},{6,7},{7,0},{8,9},{9,10},{10,1... | collective-permute-start | bytes 1179656 | tf_op jit(solution)/shard_map/ppermute | solution.py:21
  104.0 23.7 %collective-permute-start.13 = (bf16[384,512]{1,0:T(8,128)(2,1)S(1)}, bf16[384,512]{1,0:T(8,128)(2,1)}, u32[]{:S(2)}, u32[]{:S(2)}) collective-permute-start(bf16[384,512]{1,0:T(8,128)(2,1)S(1)} %bitcast.38), channel_id=1, source_target_pairs={{0,7},{1,0},{2,1},{3,2},{4,3},{5,4},{6,5},{7,6},{8,15},{9,8},{10,9... | collective-permute-start | bytes 1179656 | tf_op jit(solution)/shard_map/ppermute | solution.py:21
  108.0 67.5 %copy-start.2 = (bf16[2,96,4096]{2,1,0:T(8,128)(2,1)S(1)}, bf16[2,96,4096]{2,1,0:T(8,128)(2,1)}, u32[]{:S(2)}) copy-start(bf16[2,96,4096]{2,1,0:T(8,128)(2,1)} %up.3) | copy-start | bytes 4718596
  109.8 9.7 %collective-permute-start.4 = (bf16[296,512]{1,0:T(8,128)(2,1)S(1)}, bf16[296,512]{1,0:T(8,128)(2,1)S(1)}, u32[]{:S(2)}, u32[]{:S(2)}) collective-permute-start(bf16[296,512]{1,0:T(8,128)(2,1)S(1)} %fusion.12), channel_id=1, source_target_pairs={{0,7},{1,0},{2,1},{3,2},{4,3},{5,4},{6,5},{7,6},{8,15},{9,8},{10,9... | collective-permute-start | bytes 909320 | tf_op jit(solution)/shard_map/ppermute | solution.py:21
  112.7 25.8 %collective-permute-start.17 = (bf16[384,512]{1,0:T(8,128)(2,1)S(1)}, bf16[384,512]{1,0:T(8,128)(2,1)}, u32[]{:S(2)}, u32[]{:S(2)}) collective-permute-start(bf16[384,512]{1,0:T(8,128)(2,1)S(1)} %collective-permute-done.16.refs_5_), channel_id=1, source_target_pairs={{0,7},{1,0},{2,1},{3,2},{4,3},{5,4},{6,5},{7,6},{8,15},{9,8},{10,9... | collective-permute-start | bytes 1179656 | tf_op jit(solution)/shard_map/ppermute | solution.py:21
  115.4 27.5 %collective-permute-start.8 = (bf16[384,512]{1,0:T(8,128)(2,1)S(1)}, bf16[384,512]{1,0:T(8,128)(2,1)}, u32[]{:S(2)}, u32[]{:S(2)}) collective-permute-start(bf16[384,512]{1,0:T(8,128)(2,1)S(1)} %collective-permute-done.7.refs_2_), channel_id=1, source_target_pairs={{0,1},{1,2},{2,3},{3,4},{4,5},{5,6},{6,7},{7,0},{8,9},{9,10},{10,1... | collective-permute-start | bytes 1179656 | tf_op jit(solution)/shard_map/ppermute | solution.py:21
  119.5 14.4 %collective-permute-start.6 = (bf16[200,512]{1,0:T(8,128)(2,1)S(1)}, bf16[200,512]{1,0:T(8,128)(2,1)S(1)}, u32[]{:S(2)}, u32[]{:S(2)}) collective-permute-start(bf16[200,512]{1,0:T(8,128)(2,1)S(1)} %copy-done.31), channel_id=1, source_target_pairs={{0,6},{1,7},{2,0},{3,1},{4,2},{5,3},{6,4},{7,5},{8,14},{9,15},{10,... | collective-permute-start | bytes 614408 | tf_op jit(solution)/shard_map/ppermute | solution.py:21
  125.7 42.6 %collective-permute-start.11 = (bf16[384,512]{1,0:T(8,128)(2,1)}, bf16[384,512]{1,0:T(8,128)(2,1)}, u32[]{:S(2)}, u32[]{:S(2)}) collective-permute-start(bf16[384,512]{1,0:T(8,128)(2,1)} %collective-permute-done.10.refs_3_), channel_id=1, source_target_pairs={{0,1},{1,2},{2,3},{3,4},{4,5},{5,6},{6,7},{7,0},{8,9},{9,10},{10,1... | collective-permute-start | bytes 1179656 | tf_op jit(solution)/shard_map/ppermute | solution.py:21
  127.7 45.9 %collective-permute-start.14 = (bf16[384,512]{1,0:T(8,128)(2,1)}, bf16[384,512]{1,0:T(8,128)(2,1)}, u32[]{:S(2)}, u32[]{:S(2)}) collective-permute-start(bf16[384,512]{1,0:T(8,128)(2,1)} %collective-permute-done.13.refs_4_), channel_id=1, source_target_pairs={{0,7},{1,0},{2,1},{3,2},{4,3},{5,4},{6,5},{7,6},{8,15},{9,8},{10,9... | collective-permute-start | bytes 1179656 | tf_op jit(solution)/shard_map/ppermute | solution.py:21
  134.6 23.5 %collective-permute-start.5 = (bf16[296,512]{1,0:T(8,128)(2,1)}, bf16[296,512]{1,0:T(8,128)(2,1)}, u32[]{:S(2)}, u32[]{:S(2)}) collective-permute-start(bf16[296,512]{1,0:T(8,128)(2,1)} %fusion.11), channel_id=1, source_target_pairs={{0,5},{1,6},{2,7},{3,0},{4,1},{5,2},{6,3},{7,4},{8,13},{9,14},{10,... | collective-permute-start | bytes 909320 | tf_op jit(solution)/shard_map/ppermute | solution.py:21
  138.5 46.6 %collective-permute-start.18 = (bf16[384,512]{1,0:T(8,128)(2,1)}, bf16[384,512]{1,0:T(8,128)(2,1)}, u32[]{:S(2)}, u32[]{:S(2)}) collective-permute-start(bf16[384,512]{1,0:T(8,128)(2,1)} %collective-permute-done.17.refs_9_), channel_id=1, source_target_pairs={{0,7},{1,0},{2,1},{3,2},{4,3},{5,4},{6,5},{7,6},{8,15},{9,8},{10,9... | collective-permute-start | bytes 1179656 | tf_op jit(solution)/shard_map/ppermute | solution.py:21
  142.8 42.3 %collective-permute-start.9 = (bf16[384,512]{1,0:T(8,128)(2,1)}, bf16[384,512]{1,0:T(8,128)(2,1)}, u32[]{:S(2)}, u32[]{:S(2)}) collective-permute-start(bf16[384,512]{1,0:T(8,128)(2,1)} %collective-permute-done.8.refs_6_), channel_id=1, source_target_pairs={{0,1},{1,2},{2,3},{3,4},{4,5},{5,6},{6,7},{7,0},{8,9},{9,10},{10,1... | collective-permute-start | bytes 1179656 | tf_op jit(solution)/shard_map/ppermute | solution.py:21
  168.3 24.1 %collective-permute-start.12 = (bf16[384,512]{1,0:T(8,128)(2,1)}, bf16[384,512]{1,0:T(8,128)(2,1)}, u32[]{:S(2)}, u32[]{:S(2)}) collective-permute-start(bf16[384,512]{1,0:T(8,128)(2,1)} %collective-permute-done.11.refs_7_), channel_id=1, source_target_pairs={{0,1},{1,2},{2,3},{3,4},{4,5},{5,6},{6,7},{7,0},{8,9},{9,10},{10,1... | collective-permute-start | bytes 1179656 | tf_op jit(solution)/shard_map/ppermute | solution.py:21
  173.5 18.8 %collective-permute-start.15 = (bf16[384,512]{1,0:T(8,128)(2,1)}, bf16[384,512]{1,0:T(8,128)(2,1)}, u32[]{:S(2)}, u32[]{:S(2)}) collective-permute-start(bf16[384,512]{1,0:T(8,128)(2,1)} %collective-permute-done.14.refs_8_), channel_id=1, source_target_pairs={{0,7},{1,0},{2,1},{3,2},{4,3},{5,4},{6,5},{7,6},{8,15},{9,8},{10,9... | collective-permute-start | bytes 1179656 | tf_op jit(solution)/shard_map/ppermute | solution.py:21
  185.1 11.9 %collective-permute-start.19 = (bf16[384,512]{1,0:T(8,128)(2,1)}, bf16[384,512]{1,0:T(8,128)(2,1)}, u32[]{:S(2)}, u32[]{:S(2)}) collective-permute-start(bf16[384,512]{1,0:T(8,128)(2,1)} %collective-permute-done.9.refs_0_), channel_id=1, source_target_pairs={{0,1},{1,2},{2,3},{3,4},{4,5},{5,6},{6,7},{7,0},{8,9},{9,10},{10,1... | collective-permute-start | bytes 1179656 | tf_op jit(solution)/shard_map/ppermute | solution.py:21
  188.5 10.1 %collective-permute-start.20 = (bf16[384,512]{1,0:T(8,128)(2,1)}, bf16[384,512]{1,0:T(8,128)(2,1)}, u32[]{:S(2)}, u32[]{:S(2)}) collective-permute-start(bf16[384,512]{1,0:T(8,128)(2,1)} %collective-permute-done.18.refs_3_), channel_id=1, source_target_pairs={{0,7},{1,0},{2,1},{3,2},{4,3},{5,4},{6,5},{7,6},{8,15},{9,8},{10,9... | collective-permute-start | bytes 1179656 | tf_op jit(solution)/shard_map/ppermute | solution.py:21
  205.0 23.2 %all-to-all-start.2 = ((bf16[8,96,768]{2,1,0:T(8,128)(2,1)}), bf16[8,96,768]{2,1,0:T(8,128)(2,1)S(1)}, u32[]{:S(2)}, u32[]{:S(2)}) async-start(bf16[8,96,768]{2,1,0:T(8,128)(2,1)} %copy-done.3), calls=%async_computation.2 | async-start | bytes 2359296 | tf_op jit(solution)/shard_map/all_to_all | solution.py:29
  (33 other events, 166.4 us)
where the time goes:
time: 321 us; the launch traced here: 319 us
  blocking collectives  134 us (42%)
  starting transfers between devices  82 us (26%)
  waiting for transfers between devices  58.6 us (18%)
  local copies, waits for them, and re-layouts  25.2 us (8%)
  Pallas kernels  10.3 us (3%)
  other arithmetic  5.62 us (2%)
    all_to_all x1, blocking collectives, sent(): return lax.all_to_all(tiles, axes, split_axis=0, concat_axis=0, tiled=True)  88.3 us
    ppermute x21, starting transfers between devices, shifted(): lax.ppermute(array, 'hidden', [(i, (i + step) % devices) for i in range(d...  73.8 us
    all_to_all x1, blocking collectives, in_two_stages(): lax.all_to_all(tiles, EXPERT[k], split_axis=k, concat_axis=k, tiled=True)  45.4 us
    unnamed x68, local copies, waits for them, and re-layouts  22.8 us
    all_to_all x1, waiting for transfers between devices, in_two_stages(): lax.all_to_all(tiles, EXPERT[k], split_axis=k, concat_axis=k, tiled=True)  20.1 us
    ppermute x21, waiting for transfers between devices, shifted(): lax.ppermute(array, 'hidden', [(i, (i + step) % devices) for i in range(d...  19.5 us
    all_to_all x1, waiting for transfers between devices, sent(): return lax.all_to_all(tiles, axes, split_axis=0, concat_axis=0, tiled=True)  19 us
    pallas_call x2, Pallas kernels, add_blocks(): pl.pallas_call(body, out_shape=done if finish else shapes, in_specs=[pl.B...  6.95 us
  transfers between devices with their start and end apart: 23, of which 5 were waited for; matrix products, arithmetic and copies ran while one was open for 2% of the time, Pallas kernels for 2%

commit v1 on v0

--- a/solution.py
+++ b/solution.py
@@ -27,14 +27,6 @@
 
 def sent(tiles, axes):
     return lax.all_to_all(tiles, axes, split_axis=0, concat_axis=0, tiled=True)
-
-
-def in_two_stages(tiles):
-    shape = [lax.axis_size(a) for a in EXPERT]
-    tiles = tiles.reshape(*shape, *tiles.shape[1:])
-    for k in (1, 0):
-        tiles = lax.all_to_all(tiles, EXPERT[k], split_axis=k, concat_axis=k, tiled=True)
-    return tiles
 
 
 def route_tables(expert_ids, slot_ids, gate_num, slots):
@@ -100,6 +92,13 @@
 
     def body(turn, gate, up, gain_ref, *refs):
         block_refs, refs = list(refs[: len(pieces)]), refs[len(pieces) :]
+        refs, (landed, sems) = refs[:-2], refs[-2:]
+        moves = [
+            pltpu.make_async_copy(ref, landed.at[n], sems.at[n]) for n, ref in enumerate(block_refs)
+        ]
+        for move in moves:
+            move.start()
+        done_pieces = 0
         start_sums, start_squares = refs[:2] if before else (None, None)
         refs = refs[2:] if before else refs
         out, (sums, squares) = (refs[0], refs[1:]) if finish else (None, refs)
@@ -111,7 +110,9 @@
             cut = cut * gain_ref[d, 0:1, :]
             first = 0
             for piece in group:
-                rows = block_refs.pop(0)[...]
+                moves[done_pieces].wait()
+                rows = landed[done_pieces]
+                done_pieces += 1
                 here = pl.ds(first, piece.shape[0])
                 first += piece.shape[0]
                 product = lax.dot_general(
@@ -146,9 +147,16 @@
     return pl.pallas_call(
         body,
         out_shape=done if finish else shapes,
-        in_specs=[pl.BlockSpec(memory_space=pltpu.SMEM)] + [vmem] * (3 + len(pieces) + len(held)),
+        in_specs=[pl.BlockSpec(memory_space=pltpu.SMEM)]
+        + [vmem] * 3
+        + [pl.BlockSpec(memory_space=pltpu.HBM)] * len(pieces)
+        + [vmem] * len(held),
         out_specs=vmem if finish else [vmem] * 2,
-        scratch_shapes=[pltpu.VMEM(s.shape, s.dtype) for s in shapes] if finish else [],
+        scratch_shapes=([pltpu.VMEM(s.shape, s.dtype) for s in shapes] if finish else [])
+        + [
+            pltpu.VMEM((len(pieces), *pieces[0].shape), pieces[0].dtype),
+            pltpu.SemaphoreType.DMA((len(pieces),)),
+        ],
         compiler_params=pltpu.CompilerParams(vmem_limit_bytes=LIMIT),
         cost_estimate=pl.CostEstimate(
             flops=2 * wide * width * rows_all * count, bytes_accessed=0, transcendentals=0
@@ -203,11 +211,12 @@
     outgoing = lax.dot_general(
         placing, tokens, (((0,), (0,)), ((), ())), preferred_element_type=jnp.float32
     ).astype(jnp.bfloat16)
-    received = in_two_stages(outgoing.reshape(sources, per_source, width))
+    received = sent(outgoing.reshape(sources, per_source, width), EXPERT)
     received = received.reshape(rows_all, width)
 
     size = rows_all // HALVES
-    owner = (lax.broadcasted_iota(jnp.int32, (1, rows_all), 1) % per_source) // CAP
+    owner = (lax.broadcasted_iota(jnp.int32, (1, rows_all), 1)[0] % per_source) // CAP
+    masks = [owner == e for e in range(local)]
     halves = [received[k * size : (k + 1) * size] for k in range(HALVES)]
     blocks = [{0: half} for half in halves]
     ahead, back = list(halves), list(halves)
@@ -219,20 +228,19 @@
     held = add_blocks(
         turns, gate_proj, up_proj, gains, {d: [b[d] for b in blocks] for d in early}, None, False
     )
-    ahead[0], back[1], held = lax.optimization_barrier((ahead[0], back[1], held))
     blocks[0][far] = shifted(ahead[0], 1)
     blocks[1][far] = shifted(back[1], -1)
     late = [d for d in order if d not in early]
     copies = add_blocks(
         turns, gate_proj, up_proj, gains, {d: [b[d] for b in blocks] for d in late}, held, True
     )
-    held = (copies, down_all, weights, owner)
-    copies, down_all, weights, owner = lax.optimization_barrier(held)
+    held = (copies, down_all, weights, masks)
+    copies, down_all, weights, masks = lax.optimization_barrier(held)
     gathered = sent(copies, "hidden")
     gathered = gathered.reshape(parts * units, rows_all)
     result = jnp.zeros((rows_all, width), jnp.float32)
     for e in range(local):
-        spread = jnp.where(owner == e, gathered, jnp.zeros_like(gathered))
+        spread = jnp.where(masks[e], gathered, jnp.zeros_like(gathered))
         down = down_all[:, e * units : (e + 1) * units].reshape(parts * units, width)
         result = result + lax.dot_general(
             spread, down, (((0,), (0,)), ((), ())), preferred_element_type=jnp.float32

time: 321 us -> 311 us (0.969)
  blocking collectives: 134 us -> 90.6 us
  starting transfers between devices: 82 us -> 116 us
  local copies, waits for them, and re-layouts: 25.2 us -> 14.8 us
  waiting for transfers between devices: 58.6 us -> 65.8 us
    all_to_all x1 -> x0, blocking collectives: 45.4 us -> none  [in_two_stages(): lax.all_to_all(tiles, EXPERT[k], split_axis=k, concat_axis=k, tiled=True)]
    all_to_all x1, starting transfers between devices: 4.21 us -> 45.2 us  [sent(): return lax.all_to_all(tiles, axes, split_axis=0, concat_axis=0, tiled=True)]
    all_to_all x1 -> x0, waiting for transfers between devices: 20.1 us -> none  [in_two_stages(): lax.all_to_all(tiles, EXPERT[k], split_axis=k, concat_axis=k, tiled=True)]
    all_to_all x1, waiting for transfers between devices: 19 us -> 34.9 us  [sent(): return lax.all_to_all(tiles, axes, split_axis=0, concat_axis=0, tiled=True)]
    ppermute x21, waiting for transfers between devices: 19.5 us -> 30.9 us  [shifted(): lax.ppermute(array, 'hidden', [(i, (i + step) % devices) for i in range(d...]
    unnamed x68 -> x52, local copies, waits for them, and re-layouts: 22.8 us -> 12.9 us
    all_to_all x1 -> x0, starting transfers between devices: 4.05 us -> none  [in_two_stages(): lax.all_to_all(tiles, EXPERT[k], split_axis=k, concat_axis=k, tiled=True)]
    ppermute x21, starting transfers between devices: 73.8 us -> 70.4 us  [shifted(): lax.ppermute(array, 'hidden', [(i, (i + step) % devices) for i in range(d...]
  transfers between devices with their start and end apart: 23 -> 22, of which waited for: 5 -> 6; matrix products, arithmetic and copies ran while one was open for 2% -> 2% of each run, Pallas kernels for 2% -> 3%
where the time goes in v1:
time: 311 us; the launch traced here: 310 us
  starting transfers between devices  116 us (37%)
  blocking collectives  90.6 us (29%)
  waiting for transfers between devices  65.8 us (21%)
  local copies, waits for them, and re-layouts  14.8 us (5%)
  Pallas kernels  12 us (4%)
  other arithmetic  6.47 us (2%)
  matrix products  3.84 us (1%)
    all_to_all x2, blocking collectives, sent(): return lax.all_to_all(tiles, axes, split_axis=0, concat_axis=0, tiled=True)  90.6 us
    ppermute x21, starting transfers between devices, shifted(): lax.ppermute(array, 'hidden', [(i, (i + step) % devices) for i in range(d...  70.4 us
    all_to_all x1, starting transfers between devices, sent(): return lax.all_to_all(tiles, axes, split_axis=0, concat_axis=0, tiled=True)  45.2 us
    all_to_all x1, waiting for transfers between devices, sent(): return lax.all_to_all(tiles, axes, split_axis=0, concat_axis=0, tiled=True)  34.9 us
    ppermute x21, waiting for transfers between devices, shifted(): lax.ppermute(array, 'hidden', [(i, (i + step) % devices) for i in range(d...  30.9 us
    unnamed x52, local copies, waits for them, and re-layouts  12.9 us
    pallas_call x2, Pallas kernels, add_blocks(): pl.pallas_call(body, out_shape=done if finish else shapes, in_specs=[pl.B...  8.62 us
  transfers between devices with their start and end apart: 22, of which 6 were waited for; matrix products, arithmetic and copies ran while one was open for 2% of the time, Pallas kernels for 3%

profile of v1, /device:TPU:65, one launch (start us, length us, event | category | flops | bytes accessed | tf_op | source)
XLA Modules:
  0.0 309.8 jit_solution(12827563814252571956)
XLA Ops:
  2.8 45.2 %all-to-all-start = ((bf16[32,24,512]{2,1,0:T(8,128)(2,1)}), bf16[32,24,512]{2,1,0:T(8,128)(2,1)S(1)}, u32[]{:S(2)}, u32[]{:S(2)}) async-start(bf16[32,24,512]{2,1,0:T(8,128)(2,1)} %bitcast.17), calls=%async_computation | async-start | bytes 1572864 | tf_op jit(solution)/shard_map/all_to_all | solution.py:29
  50.1 3.2 %collective-permute-start = (bf16[200,512]{1,0:T(8,128)(2,1)}, bf16[200,512]{1,0:T(8,128)(2,1)S(1)}, u32[]{:S(2)}, u32[]{:S(2)}) collective-permute-start(bf16[200,512]{1,0:T(8,128)(2,1)} %get-tuple-element.35), channel_id=1, source_target_pairs={{0,1},{1,2},{2,3},{3,4},{4,5},{5,6},{6,7},{7,0},{8,9},{9,10},{10,1... | collective-permute-start | bytes 614408 | tf_op jit(solution)/shard_map/ppermute | solution.py:21
  53.3 4.4 %collective-permute-start.1 = (bf16[200,512]{1,0:T(8,128)(2,1)}, bf16[200,512]{1,0:T(8,128)(2,1)S(1)}, u32[]{:S(2)}, u32[]{:S(2)}) collective-permute-start(bf16[200,512]{1,0:T(8,128)(2,1)} %get-tuple-element.36), channel_id=1, source_target_pairs={{0,2},{1,3},{2,4},{3,5},{4,6},{5,7},{6,0},{7,1},{8,10},{9,11},{10,... | collective-permute-start | bytes 614408 | tf_op jit(solution)/shard_map/ppermute | solution.py:21
  57.7 34.9 %all-to-all-done = bf16[32,24,512]{2,1,0:T(8,128)(2,1)S(1)} async-done(((bf16[32,24,512]{2,1,0:T(8,128)(2,1)}), bf16[32,24,512]{2,1,0:T(8,128)(2,1)S(1)}, u32[]{:S(2)}, u32[]{:S(2)}) %all-to-all-start) | async-done | bytes 786464 | tf_op jit(solution)/shard_map/all_to_all | solution.py:29
  92.6 5.4 %collective-permute-start.16 = (bf16[384,512]{1,0:T(8,128)(2,1)S(1)}, bf16[384,512]{1,0:T(8,128)(2,1)S(1)}, u32[]{:S(2)}, u32[]{:S(2)}) collective-permute-start(bf16[384,512]{1,0:T(8,128)(2,1)S(1)} %bitcast.34), channel_id=1, source_target_pairs={{0,7},{1,0},{2,1},{3,2},{4,3},{5,4},{6,5},{7,6},{8,15},{9,8},{10,9... | collective-permute-start | bytes 1179656 | tf_op jit(solution)/shard_map/ppermute | solution.py:21
  100.1 5.6 %collective-permute-start.3 = (bf16[104,512]{1,0:T(8,128)(2,1)S(1)}, bf16[104,512]{1,0:T(8,128)(2,1)S(1)}, u32[]{:S(2)}, u32[]{:S(2)}) collective-permute-start(bf16[104,512]{1,0:T(8,128)(2,1)S(1)} %pad_maximum_fusion.7), channel_id=1, source_target_pairs={{0,4},{1,5},{2,6},{3,7},{4,0},{5,1},{6,2},{7,3},{8,12},{9,13},{10,... | collective-permute-start | bytes 319496 | tf_op jit(solution)/shard_map/ppermute | solution.py:21
  105.7 10.7 %collective-permute-done.3.refs_4_ = bf16[104,512]{1,0:T(8,128)(2,1)S(1)} collective-permute-done((bf16[104,512]{1,0:T(8,128)(2,1)S(1)}, bf16[104,512]{1,0:T(8,128)(2,1)S(1)}, u32[]{:S(2)}, u32[]{:S(2)}) %collective-permute-start.3) | collective-permute-done | bytes 106528 | tf_op jit(solution)/shard_map/ppermute | solution.py:21
  119.0 2.9 collective-permute-start.10
  122.6 3.7 %collective-permute-start.13 = (bf16[384,512]{1,0:T(8,128)(2,1)S(1)}, bf16[384,512]{1,0:T(8,128)(2,1)}, u32[]{:S(2)}, u32[]{:S(2)}) collective-permute-start(bf16[384,512]{1,0:T(8,128)(2,1)S(1)} %bitcast.38), channel_id=1, source_target_pairs={{0,7},{1,0},{2,1},{3,2},{4,3},{5,4},{6,5},{7,6},{8,15},{9,8},{10,9... | collective-permute-start | bytes 1179656 | tf_op jit(solution)/shard_map/ppermute | solution.py:21
  128.2 3.4 %collective-permute-start.8 = (bf16[384,512]{1,0:T(8,128)(2,1)S(1)}, bf16[384,512]{1,0:T(8,128)(2,1)}, u32[]{:S(2)}, u32[]{:S(2)}) collective-permute-start(bf16[384,512]{1,0:T(8,128)(2,1)S(1)} %collective-permute-done.7.refs_2_), channel_id=1, source_target_pairs={{0,1},{1,2},{2,3},{3,4},{4,5},{5,6},{6,7},{7,0},{8,9},{9,10},{10,1... | collective-permute-start | bytes 1179656 | tf_op jit(solution)/shard_map/ppermute | solution.py:21
  137.9 9.5 %collective-permute-done.4.refs_7_ = bf16[296,512]{1,0:T(8,128)(2,1)S(1)} collective-permute-done((bf16[296,512]{1,0:T(8,128)(2,1)S(1)}, bf16[296,512]{1,0:T(8,128)(2,1)S(1)}, u32[]{:S(2)}, u32[]{:S(2)}) %collective-permute-start.4) | collective-permute-done | bytes 303136 | tf_op jit(solution)/shard_map/ppermute | solution.py:21
  147.4 4.0 %collective-permute-start.6 = (bf16[200,512]{1,0:T(8,128)(2,1)S(1)}, bf16[200,512]{1,0:T(8,128)(2,1)S(1)}, u32[]{:S(2)}, u32[]{:S(2)}) collective-permute-start(bf16[200,512]{1,0:T(8,128)(2,1)S(1)} %copy-done.23), channel_id=1, source_target_pairs={{0,6},{1,7},{2,0},{3,1},{4,2},{5,3},{6,4},{7,5},{8,14},{9,15},{10,... | collective-permute-start | bytes 614408 | tf_op jit(solution)/shard_map/ppermute | solution.py:21
  151.4 4.5 %collective-permute-start.11 = (bf16[384,512]{1,0:T(8,128)(2,1)}, bf16[384,512]{1,0:T(8,128)(2,1)}, u32[]{:S(2)}, u32[]{:S(2)}) collective-permute-start(bf16[384,512]{1,0:T(8,128)(2,1)} %collective-permute-done.10.refs_3_), channel_id=1, source_target_pairs={{0,1},{1,2},{2,3},{3,4},{4,5},{5,6},{6,7},{7,0},{8,9},{9,10},{10,1... | collective-permute-start | bytes 1179656 | tf_op jit(solution)/shard_map/ppermute | solution.py:21
  158.0 3.2 %collective-permute-start.9 = (bf16[384,512]{1,0:T(8,128)(2,1)}, bf16[384,512]{1,0:T(8,128)(2,1)}, u32[]{:S(2)}, u32[]{:S(2)}) collective-permute-start(bf16[384,512]{1,0:T(8,128)(2,1)} %collective-permute-done.8.refs_6_), channel_id=1, source_target_pairs={{0,1},{1,2},{2,3},{3,4},{4,5},{5,6},{6,7},{7,0},{8,9},{9,10},{10,1... | collective-permute-start | bytes 1179656 | tf_op jit(solution)/shard_map/ppermute | solution.py:21
  161.3 3.3 %collective-permute-start.18 = (bf16[384,512]{1,0:T(8,128)(2,1)}, bf16[384,512]{1,0:T(8,128)(2,1)}, u32[]{:S(2)}, u32[]{:S(2)}) collective-permute-start(bf16[384,512]{1,0:T(8,128)(2,1)} %collective-permute-done.17.refs_9_), channel_id=1, source_target_pairs={{0,7},{1,0},{2,1},{3,2},{4,3},{5,4},{6,5},{7,6},{8,15},{9,8},{10,9... | collective-permute-start | bytes 1179656 | tf_op jit(solution)/shard_map/ppermute | solution.py:21
  167.7 3.8 %collective-permute-start.5 = (bf16[296,512]{1,0:T(8,128)(2,1)}, bf16[296,512]{1,0:T(8,128)(2,1)}, u32[]{:S(2)}, u32[]{:S(2)}) collective-permute-start(bf16[296,512]{1,0:T(8,128)(2,1)} %fusion.11), channel_id=1, source_target_pairs={{0,5},{1,6},{2,7},{3,0},{4,1},{5,2},{6,3},{7,4},{8,13},{9,14},{10,... | collective-permute-start | bytes 909320 | tf_op jit(solution)/shard_map/ppermute | solution.py:21
  174.3 4.6 %collective-permute-start.15 = (bf16[384,512]{1,0:T(8,128)(2,1)}, bf16[384,512]{1,0:T(8,128)(2,1)S(1)}, u32[]{:S(2)}, u32[]{:S(2)}) collective-permute-start(bf16[384,512]{1,0:T(8,128)(2,1)} %collective-permute-done.14.refs_8_), channel_id=1, source_target_pairs={{0,7},{1,0},{2,1},{3,2},{4,3},{5,4},{6,5},{7,6},{8,15},{9,8},{10,9... | collective-permute-start | bytes 1179656 | tf_op jit(solution)/shard_map/ppermute | solution.py:21
  180.9 4.6 %collective-permute-start.20 = (bf16[384,512]{1,0:T(8,128)(2,1)}, bf16[384,512]{1,0:T(8,128)(2,1)S(1)}, u32[]{:S(2)}, u32[]{:S(2)}) collective-permute-start(bf16[384,512]{1,0:T(8,128)(2,1)} %collective-permute-done.18.refs_3_), channel_id=1, source_target_pairs={{0,7},{1,0},{2,1},{3,2},{4,3},{5,4},{6,5},{7,6},{8,15},{9,8},{10,9... | collective-permute-start | bytes 1179656 | tf_op jit(solution)/shard_map/ppermute | solution.py:21
  186.9 6.7 %collective-permute-done.5.refs_5_ = bf16[296,512]{1,0:T(8,128)(2,1)} collective-permute-done((bf16[296,512]{1,0:T(8,128)(2,1)}, bf16[296,512]{1,0:T(8,128)(2,1)}, u32[]{:S(2)}, u32[]{:S(2)}) %collective-permute-start.5) | collective-permute-done | bytes 303136 | tf_op jit(solution)/shard_map/ppermute | solution.py:21
  198.2 3.4 %shard_map.82 = (bf16[8,192,512]{2,1,0:T(8,128)(2,1)S(1)}, bf16[8,8,512]{2,1,0:T(8,128)(2,1)S(1)}) custom-call(s32[8]{0:T(128)S(1)} %stack.35.turn, bf16[200,512]{1,0:T(8,128)(2,1)S(1)} %get-tuple-element.38.refs_0_, bf16[200,512]{1,0:T(8,128)(2,1)S(1)} %copy-done.14, bf16[200,512]{1,0:T(8,128)(2,1)S(1)} %copy-done.16, bf16[200,512]{1,0:T(8,128)(2,1)S(1)} %copy-done.18, ...), custom_call_target="tpu_custom_call" | custom-call | flops 100000000 | bytes 3145728 | tf_op jit(solution)/shard_map/pallas_call | solution.py:64
  205.6 4.8 %shard_map.83 = (f32[384,768]{1,0:T(8,128)S(1)}, f32[768,128]{1,0:T(8,128)S(1)}) custom-call(s32[8]{0:T(128)S(1)} %stack.35.turn, bf16[2,96,4096]{2,1,0:T(8,128)(2,1)S(1)} %copy-done.1, bf16[2,96,4096]{2,1,0:T(8,128)(2,1)S(1)} %copy-done.2, bf16[8,8,512]{2,1,0:T(8,128)(2,1)S(1)} %get-tuple-element.14.gain_ref, bf16[384,512]{1,0:T(8,128)(2,1)S(1)} %bitcast.39, ...), custom_call_target="tpu_custom_call" | custom-call | flops 1509949440 | tf_op jit(solution)/shard_map/pallas_call | solution.py:147
  212.8 3.8 %shard_map.84 = bf16[8,96,768]{2,1,0:T(8,128)(2,1)S(1)} custom-call(s32[8]{0:T(128)S(1)} %stack.35.turn, bf16[2,96,4096]{2,1,0:T(8,128)(2,1)S(1)} %copy-done.1, bf16[2,96,4096]{2,1,0:T(8,128)(2,1)S(1)} %copy-done.2, bf16[8,8,512]{2,1,0:T(8,128)(2,1)S(1)} %get-tuple-element.14.gain_ref, bf16[384,512]{1,0:T(8,128)(2,1)} %collective-permute-done.9.refs_0_, ...), custom_call_target="tpu_custom_call" | custom-call | flops 905969664 | tf_op jit(solution)/shard_map/pallas_call | solution.py:147
  216.6 34.7 %all_to_all.15 = bf16[8,96,768]{2,1,0:T(8,128)(2,1)S(1)} all-to-all(bf16[8,96,768]{2,1,0:T(8,128)(2,1)S(1)} %shard_map.84), channel_id=1, replica_groups=mesh['groups'=2,'expert_0'=16,'expert_1'=2,'hidden'=8] {'hidden'}, dimensions={0} | all-to-all | bytes 2359296 | tf_op jit(solution)/shard_map/all_to_all | solution.py:29
  252.9 55.9 %all_to_all.16 = bf16[32,24,512]{2,1,0:T(8,128)(2,1)S(1)} all-to-all(bf16[32,24,512]{2,1,0:T(8,128)(2,1)S(1)} %bitcast.41), channel_id=1, replica_groups=mesh['groups'=2,'expert_0'=16,'expert_1'=2,'hidden'=8] {'expert_0','expe..., dimensions={0} | all-to-all | bytes 1572864 | tf_op jit(solution)/shard_map/all_to_all | solution.py:29
  (98 shorter events, 43.0 us)
Async XLA Ops:
  2.8 89.8 %all-to-all-start = ((bf16[32,24,512]{2,1,0:T(8,128)(2,1)}), bf16[32,24,512]{2,1,0:T(8,128)(2,1)S(1)}, u32[]{:S(2)}, u32[]{:S(2)}) async-start(bf16[32,24,512]{2,1,0:T(8,128)(2,1)} %bitcast.17), calls=%async_computation | async-start | bytes 1572864 | tf_op jit(solution)/shard_map/all_to_all | solution.py:29
  50.1 68.2 %collective-permute-start = (bf16[200,512]{1,0:T(8,128)(2,1)}, bf16[200,512]{1,0:T(8,128)(2,1)S(1)}, u32[]{:S(2)}, u32[]{:S(2)}) collective-permute-start(bf16[200,512]{1,0:T(8,128)(2,1)} %get-tuple-element.35), channel_id=1, source_target_pairs={{0,1},{1,2},{2,3},{3,4},{4,5},{5,6},{6,7},{7,0},{8,9},{9,10},{10,1... | collective-permute-start | bytes 614408 | tf_op jit(solution)/shard_map/ppermute | solution.py:21
  53.3 68.6 %collective-permute-start.1 = (bf16[200,512]{1,0:T(8,128)(2,1)}, bf16[200,512]{1,0:T(8,128)(2,1)S(1)}, u32[]{:S(2)}, u32[]{:S(2)}) collective-permute-start(bf16[200,512]{1,0:T(8,128)(2,1)} %get-tuple-element.36), channel_id=1, source_target_pairs={{0,2},{1,3},{2,4},{3,5},{4,6},{5,7},{6,0},{7,1},{8,10},{9,11},{10,... | collective-permute-start | bytes 614408 | tf_op jit(solution)/shard_map/ppermute | solution.py:21
  57.7 113.8 %copy-start.24 = (s32[64,8]{0,1:T(8,128)S(1)}, s32[64,8]{0,1:T(8,128)}, u32[]{:S(2)}) copy-start(s32[64,8]{0,1:T(8,128)} %param.15) | copy-start | bytes 6148
  92.6 33.6 %collective-permute-start.16 = (bf16[384,512]{1,0:T(8,128)(2,1)S(1)}, bf16[384,512]{1,0:T(8,128)(2,1)S(1)}, u32[]{:S(2)}, u32[]{:S(2)}) collective-permute-start(bf16[384,512]{1,0:T(8,128)(2,1)S(1)} %bitcast.34), channel_id=1, source_target_pairs={{0,7},{1,0},{2,1},{3,2},{4,3},{5,4},{6,5},{7,6},{8,15},{9,8},{10,9... | collective-permute-start | bytes 1179656 | tf_op jit(solution)/shard_map/ppermute | solution.py:21
  98.1 30.1 %collective-permute-start.7 = (bf16[384,512]{1,0:T(8,128)(2,1)S(1)}, bf16[384,512]{1,0:T(8,128)(2,1)S(1)}, u32[]{:S(2)}, u32[]{:S(2)}) collective-permute-start(bf16[384,512]{1,0:T(8,128)(2,1)S(1)} %bitcast.37), channel_id=1, source_target_pairs={{0,1},{1,2},{2,3},{3,4},{4,5},{5,6},{6,7},{7,0},{8,9},{9,10},{10,1... | collective-permute-start | bytes 1179656 | tf_op jit(solution)/shard_map/ppermute | solution.py:21
  100.1 16.3 %collective-permute-start.3 = (bf16[104,512]{1,0:T(8,128)(2,1)S(1)}, bf16[104,512]{1,0:T(8,128)(2,1)S(1)}, u32[]{:S(2)}, u32[]{:S(2)}) collective-permute-start(bf16[104,512]{1,0:T(8,128)(2,1)S(1)} %pad_maximum_fusion.7), channel_id=1, source_target_pairs={{0,4},{1,5},{2,6},{3,7},{4,0},{5,1},{6,2},{7,3},{8,12},{9,13},{10,... | collective-permute-start | bytes 319496 | tf_op jit(solution)/shard_map/ppermute | solution.py:21
  116.4 18.9 %collective-permute-start.2 = (bf16[200,512]{1,0:T(8,128)(2,1)}, bf16[200,512]{1,0:T(8,128)(2,1)S(1)}, u32[]{:S(2)}, u32[]{:S(2)}) collective-permute-start(bf16[200,512]{1,0:T(8,128)(2,1)} %get-tuple-element.37), channel_id=1, source_target_pairs={{0,3},{1,4},{2,5},{3,6},{4,7},{5,0},{6,1},{7,2},{8,11},{9,12},{10,... | collective-permute-start | bytes 614408 | tf_op jit(solution)/shard_map/ppermute | solution.py:21
  119.0 32.4 %collective-permute-start.10 = (bf16[384,512]{1,0:T(8,128)(2,1)S(1)}, bf16[384,512]{1,0:T(8,128)(2,1)}, u32[]{:S(2)}, u32[]{:S(2)}) collective-permute-start(bf16[384,512]{1,0:T(8,128)(2,1)S(1)} %bitcast.35), channel_id=1, source_target_pairs={{0,1},{1,2},{2,3},{3,4},{4,5},{5,6},{6,7},{7,0},{8,9},{9,10},{10,1... | collective-permute-start | bytes 1179656 | tf_op jit(solution)/shard_map/ppermute | solution.py:21
  122.6 33.3 %collective-permute-start.13 = (bf16[384,512]{1,0:T(8,128)(2,1)S(1)}, bf16[384,512]{1,0:T(8,128)(2,1)}, u32[]{:S(2)}, u32[]{:S(2)}) collective-permute-start(bf16[384,512]{1,0:T(8,128)(2,1)S(1)} %bitcast.38), channel_id=1, source_target_pairs={{0,7},{1,0},{2,1},{3,2},{4,3},{5,4},{6,5},{7,6},{8,15},{9,8},{10,9... | collective-permute-start | bytes 1179656 | tf_op jit(solution)/shard_map/ppermute | solution.py:21
  126.3 35.0 %collective-permute-start.17 = (bf16[384,512]{1,0:T(8,128)(2,1)S(1)}, bf16[384,512]{1,0:T(8,128)(2,1)}, u32[]{:S(2)}, u32[]{:S(2)}) collective-permute-start(bf16[384,512]{1,0:T(8,128)(2,1)S(1)} %collective-permute-done.16.refs_5_), channel_id=1, source_target_pairs={{0,7},{1,0},{2,1},{3,2},{4,3},{5,4},{6,5},{7,6},{8,15},{9,8},{10,9... | collective-permute-start | bytes 1179656 | tf_op jit(solution)/shard_map/ppermute | solution.py:21
  128.2 29.8 %collective-permute-start.8 = (bf16[384,512]{1,0:T(8,128)(2,1)S(1)}, bf16[384,512]{1,0:T(8,128)(2,1)}, u32[]{:S(2)}, u32[]{:S(2)}) collective-permute-start(bf16[384,512]{1,0:T(8,128)(2,1)S(1)} %collective-permute-done.7.refs_2_), channel_id=1, source_target_pairs={{0,1},{1,2},{2,3},{3,4},{4,5},{5,6},{6,7},{7,0},{8,9},{9,10},{10,1... | collective-permute-start | bytes 1179656 | tf_op jit(solution)/shard_map/ppermute | solution.py:21
  132.4 69.3 %copy-start.2 = (bf16[2,96,4096]{2,1,0:T(8,128)(2,1)S(1)}, bf16[2,96,4096]{2,1,0:T(8,128)(2,1)}, u32[]{:S(2)}) copy-start(bf16[2,96,4096]{2,1,0:T(8,128)(2,1)} %up.3) | copy-start | bytes 4718596
  136.0 11.4 %collective-permute-start.4 = (bf16[296,512]{1,0:T(8,128)(2,1)S(1)}, bf16[296,512]{1,0:T(8,128)(2,1)S(1)}, u32[]{:S(2)}, u32[]{:S(2)}) collective-permute-start(bf16[296,512]{1,0:T(8,128)(2,1)S(1)} %fusion.12), channel_id=1, source_target_pairs={{0,7},{1,0},{2,1},{3,2},{4,3},{5,4},{6,5},{7,6},{8,15},{9,8},{10,9... | collective-permute-start | bytes 909320 | tf_op jit(solution)/shard_map/ppermute | solution.py:21
  147.4 19.6 %collective-permute-start.6 = (bf16[200,512]{1,0:T(8,128)(2,1)S(1)}, bf16[200,512]{1,0:T(8,128)(2,1)S(1)}, u32[]{:S(2)}, u32[]{:S(2)}) collective-permute-start(bf16[200,512]{1,0:T(8,128)(2,1)S(1)} %copy-done.23), channel_id=1, source_target_pairs={{0,6},{1,7},{2,0},{3,1},{4,2},{5,3},{6,4},{7,5},{8,14},{9,15},{10,... | collective-permute-start | bytes 614408 | tf_op jit(solution)/shard_map/ppermute | solution.py:21
  151.4 20.9 %collective-permute-start.11 = (bf16[384,512]{1,0:T(8,128)(2,1)}, bf16[384,512]{1,0:T(8,128)(2,1)}, u32[]{:S(2)}, u32[]{:S(2)}) collective-permute-start(bf16[384,512]{1,0:T(8,128)(2,1)} %collective-permute-done.10.refs_3_), channel_id=1, source_target_pairs={{0,1},{1,2},{2,3},{3,4},{4,5},{5,6},{6,7},{7,0},{8,9},{9,10},{10,1... | collective-permute-start | bytes 1179656 | tf_op jit(solution)/shard_map/ppermute | solution.py:21
  155.9 18.4 %collective-permute-start.14 = (bf16[384,512]{1,0:T(8,128)(2,1)}, bf16[384,512]{1,0:T(8,128)(2,1)}, u32[]{:S(2)}, u32[]{:S(2)}) collective-permute-start(bf16[384,512]{1,0:T(8,128)(2,1)} %collective-permute-done.13.refs_4_), channel_id=1, source_target_pairs={{0,7},{1,0},{2,1},{3,2},{4,3},{5,4},{6,5},{7,6},{8,15},{9,8},{10,9... | collective-permute-start | bytes 1179656 | tf_op jit(solution)/shard_map/ppermute | solution.py:21
  158.0 20.9 %collective-permute-start.9 = (bf16[384,512]{1,0:T(8,128)(2,1)}, bf16[384,512]{1,0:T(8,128)(2,1)}, u32[]{:S(2)}, u32[]{:S(2)}) collective-permute-start(bf16[384,512]{1,0:T(8,128)(2,1)} %collective-permute-done.8.refs_6_), channel_id=1, source_target_pairs={{0,1},{1,2},{2,3},{3,4},{4,5},{5,6},{6,7},{7,0},{8,9},{9,10},{10,1... | collective-permute-start | bytes 1179656 | tf_op jit(solution)/shard_map/ppermute | solution.py:21
  161.3 19.6 %collective-permute-start.18 = (bf16[384,512]{1,0:T(8,128)(2,1)}, bf16[384,512]{1,0:T(8,128)(2,1)}, u32[]{:S(2)}, u32[]{:S(2)}) collective-permute-start(bf16[384,512]{1,0:T(8,128)(2,1)} %collective-permute-done.17.refs_9_), channel_id=1, source_target_pairs={{0,7},{1,0},{2,1},{3,2},{4,3},{5,4},{6,5},{7,6},{8,15},{9,8},{10,9... | collective-permute-start | bytes 1179656 | tf_op jit(solution)/shard_map/ppermute | solution.py:21
  167.7 25.9 %collective-permute-start.5 = (bf16[296,512]{1,0:T(8,128)(2,1)}, bf16[296,512]{1,0:T(8,128)(2,1)}, u32[]{:S(2)}, u32[]{:S(2)}) collective-permute-start(bf16[296,512]{1,0:T(8,128)(2,1)} %fusion.11), channel_id=1, source_target_pairs={{0,5},{1,6},{2,7},{3,0},{4,1},{5,2},{6,3},{7,4},{8,13},{9,14},{10,... | collective-permute-start | bytes 909320 | tf_op jit(solution)/shard_map/ppermute | solution.py:21
  172.3 38.1 %collective-permute-start.12 = (bf16[384,512]{1,0:T(8,128)(2,1)}, bf16[384,512]{1,0:T(8,128)(2,1)S(1)}, u32[]{:S(2)}, u32[]{:S(2)}) collective-permute-start(bf16[384,512]{1,0:T(8,128)(2,1)} %collective-permute-done.11.refs_7_), channel_id=1, source_target_pairs={{0,1},{1,2},{2,3},{3,4},{4,5},{5,6},{6,7},{7,0},{8,9},{9,10},{10,1... | collective-permute-start | bytes 1179656 | tf_op jit(solution)/shard_map/ppermute | solution.py:21
  174.3 36.1 %collective-permute-start.15 = (bf16[384,512]{1,0:T(8,128)(2,1)}, bf16[384,512]{1,0:T(8,128)(2,1)S(1)}, u32[]{:S(2)}, u32[]{:S(2)}) collective-permute-start(bf16[384,512]{1,0:T(8,128)(2,1)} %collective-permute-done.14.refs_8_), channel_id=1, source_target_pairs={{0,7},{1,0},{2,1},{3,2},{4,3},{5,4},{6,5},{7,6},{8,15},{9,8},{10,9... | collective-permute-start | bytes 1179656 | tf_op jit(solution)/shard_map/ppermute | solution.py:21
  178.9 31.5 %collective-permute-start.19 = (bf16[384,512]{1,0:T(8,128)(2,1)}, bf16[384,512]{1,0:T(8,128)(2,1)S(1)}, u32[]{:S(2)}, u32[]{:S(2)}) collective-permute-start(bf16[384,512]{1,0:T(8,128)(2,1)} %collective-permute-done.9.refs_0_), channel_id=1, source_target_pairs={{0,1},{1,2},{2,3},{3,4},{4,5},{5,6},{6,7},{7,0},{8,9},{9,10},{10,1... | collective-permute-start | bytes 1179656 | tf_op jit(solution)/shard_map/ppermute | solution.py:21
  180.9 31.9 %collective-permute-start.20 = (bf16[384,512]{1,0:T(8,128)(2,1)}, bf16[384,512]{1,0:T(8,128)(2,1)S(1)}, u32[]{:S(2)}, u32[]{:S(2)}) collective-permute-start(bf16[384,512]{1,0:T(8,128)(2,1)} %collective-permute-done.18.refs_3_), channel_id=1, source_target_pairs={{0,7},{1,0},{2,1},{3,2},{4,3},{5,4},{6,5},{7,6},{8,15},{9,8},{10,9... | collective-permute-start | bytes 1179656 | tf_op jit(solution)/shard_map/ppermute | solution.py:21
  (24 other events, 371.8 us)

commit v2 on v1

--- a/solution.py
+++ b/solution.py
@@ -49,10 +49,10 @@
         return [array is known for known in arrays].index(True)
 
     def body(turn, *refs):
-        sources, (down, gains, sems) = refs[: len(arrays)], refs[len(arrays) :]
+        sources, (down, sems) = refs[: len(arrays)], refs[len(arrays) :]
         moves = []
         for n, (d, array, low, at, count) in enumerate(pieces):
-            target = gains.at[d] if at is None else down.at[turn[d], pl.ds(at, count)]
+            target = down.at[turn[d], pl.ds(at, count)]
             source = sources[place(array)].at[pl.ds(low, count)]
             moves.append(pltpu.make_async_copy(source, target, sems.at[n]))
         for move in moves:
@@ -60,16 +60,12 @@
         for move in moves:
             move.wait()
 
-    vmem = pl.BlockSpec(memory_space=pltpu.VMEM)
     return pl.pallas_call(
         body,
-        out_shape=[
-            jax.ShapeDtypeStruct((parts, rows, width), jnp.bfloat16),
-            jax.ShapeDtypeStruct((parts, 8, width), jnp.bfloat16),
-        ],
+        out_shape=jax.ShapeDtypeStruct((parts, rows, width), jnp.bfloat16),
         in_specs=[pl.BlockSpec(memory_space=pltpu.SMEM)]
         + [pl.BlockSpec(memory_space=pltpu.HBM)] * len(arrays),
-        out_specs=[vmem] * 2,
+        out_specs=pl.BlockSpec(memory_space=pltpu.VMEM),
         scratch_shapes=[pltpu.SemaphoreType.DMA((len(pieces),))],
         compiler_params=pltpu.CompilerParams(vmem_limit_bytes=LIMIT),
         cost_estimate=pl.CostEstimate(
@@ -80,9 +76,11 @@
 
 def add_blocks(turns, gate_proj, up_proj, gains, blocks, before, finish):
     local, units, features = gate_proj.shape
-    parts, _, width = gains.shape
     count = len(blocks)
     pieces = [piece for group in blocks.values() for piece in group]
+    width = pieces[0].shape[1]
+    parts = features // width
+    gain_from = [gains[d] for d in blocks]
     rows_all = sum(piece.shape[0] for piece in pieces) // count
     wide = 2 * local * units
     shapes = [
@@ -90,13 +88,18 @@
         jax.ShapeDtypeStruct((rows_all, 128), jnp.float32),
     ]
 
-    def body(turn, gate, up, gain_ref, *refs):
-        block_refs, refs = list(refs[: len(pieces)]), refs[len(pieces) :]
-        refs, (landed, sems) = refs[:-2], refs[-2:]
+    def body(turn, gate, up, *refs):
+        gain_refs, refs = refs[:count], refs[count:]
+        block_refs, refs = refs[: len(pieces)], refs[len(pieces) :]
+        refs, (landed, sems, gain_rows, gain_sems) = refs[:-4], refs[-4:]
+        gain_moves = [
+            pltpu.make_async_copy(ref.at[pl.ds(low, 8)], gain_rows.at[n], gain_sems.at[n])
+            for n, (ref, (_, low)) in enumerate(zip(gain_refs, gain_from))
+        ]
         moves = [
             pltpu.make_async_copy(ref, landed.at[n], sems.at[n]) for n, ref in enumerate(block_refs)
         ]
-        for move in moves:
+        for move in gain_moves + moves:
             move.start()
         done_pieces = 0
         start_sums, start_squares = refs[:2] if before else (None, None)
@@ -107,7 +110,8 @@
             cut = jnp.concatenate(
                 [w[e, :, pl.ds(start, width)] for w in (gate, up) for e in range(local)], axis=0
             )
-            cut = cut * gain_ref[d, 0:1, :]
+            gain_moves[n].wait()
+            cut = cut * gain_rows[n, 0:1, :]
             first = 0
             for piece in group:
                 moves[done_pieces].wait()
@@ -148,20 +152,22 @@
         body,
         out_shape=done if finish else shapes,
         in_specs=[pl.BlockSpec(memory_space=pltpu.SMEM)]
-        + [vmem] * 3
-        + [pl.BlockSpec(memory_space=pltpu.HBM)] * len(pieces)
+        + [vmem] * 2
+        + [pl.BlockSpec(memory_space=pltpu.HBM)] * (count + len(pieces))
         + [vmem] * len(held),
         out_specs=vmem if finish else [vmem] * 2,
         scratch_shapes=([pltpu.VMEM(s.shape, s.dtype) for s in shapes] if finish else [])
         + [
             pltpu.VMEM((len(pieces), *pieces[0].shape), pieces[0].dtype),
             pltpu.SemaphoreType.DMA((len(pieces),)),
+            pltpu.VMEM((count, 8, width), pieces[0].dtype),
+            pltpu.SemaphoreType.DMA((count,)),
         ],
         compiler_params=pltpu.CompilerParams(vmem_limit_bytes=LIMIT),
         cost_estimate=pl.CostEstimate(
             flops=2 * wide * width * rows_all * count, bytes_accessed=0, transcendentals=0
         ),
-    )(turns, gate_proj, up_proj, gains, *pieces, *held)
+    )(turns, gate_proj, up_proj, *[array for array, _ in gain_from], *pieces, *held)
 
 
 def layer(tokens, norm_gain, gate_proj, up_proj, down_proj, expert_ids, slot_ids, gate_num):
@@ -200,12 +206,11 @@
         jnp.concatenate([cut_by_shift[three], first[end:]], axis=0), three
     )
     turns = jnp.stack([(here - d + parts) % parts for d in range(parts)]).astype(jnp.int32)
-    pieces = []
-    for d, cut in enumerate(cut_by_shift):
-        pieces.append((d, cut, 0, 0, kept if d == far else down_rows))
-        pieces.append((d, cut, kept if d == far else down_rows, None, 8))
+    pieces = [
+        (d, cut, 0, 0, kept if d == far else down_rows) for d, cut in enumerate(cut_by_shift)
+    ]
     pieces.append((far, cut_by_shift[three], end, kept, units))
-    down_all, gains = unpacked(turns, pieces, parts, down_rows, width)
+    gains = [(cut, kept if d == far else down_rows) for d, cut in enumerate(cut_by_shift)]
 
     placing, weights = route_tables(expert_ids, slot_ids, gate_num, rows_all)
     outgoing = lax.dot_general(
@@ -234,8 +239,9 @@
     copies = add_blocks(
         turns, gate_proj, up_proj, gains, {d: [b[d] for b in blocks] for d in late}, held, True
     )
-    held = (copies, down_all, weights, masks)
-    copies, down_all, weights, masks = lax.optimization_barrier(held)
+    copies, weights, masks = lax.optimization_barrier((copies, weights, masks))
+    turns, _ = lax.optimization_barrier((turns, copies))
+    down_all = unpacked(turns, pieces, parts, down_rows, width)
     gathered = sent(copies, "hidden")
     gathered = gathered.reshape(parts * units, rows_all)
     result = jnp.zeros((rows_all, width), jnp.float32)

time: 311 us -> 313 us (level)
  blocking collectives: 90.6 us -> 48.7 us
  waiting for transfers between devices: 65.8 us -> 97.6 us
  local copies, waits for them, and re-layouts: 14.8 us -> 20 us
    all_to_all x2 -> x1, blocking collectives: 90.6 us -> 48.7 us  [sent(): return lax.all_to_all(tiles, axes, split_axis=0, concat_axis=0, tiled=True)]
    all_to_all x1 -> x2, waiting for transfers between devices: 34.9 us -> 64.8 us  [sent(): return lax.all_to_all(tiles, axes, split_axis=0, concat_axis=0, tiled=True)]
    all_to_all x1 -> x2, starting transfers between devices: 45.2 us -> 50.9 us  [sent(): return lax.all_to_all(tiles, axes, split_axis=0, concat_axis=0, tiled=True)]
    unnamed x52 -> x68, local copies, waits for them, and re-layouts: 12.9 us -> 16 us
  transfers between devices with their start and end apart: 22 -> 23, of which waited for: 6 -> 6; matrix products, arithmetic and copies ran while one was open for 2% -> 3% of each run, Pallas kernels for 3% -> 3%
where the time goes in v2:
time: 313 us; the launch traced here: 311 us
  starting transfers between devices  119 us (38%)
  waiting for transfers between devices  97.6 us (31%)
  blocking collectives  48.7 us (16%)
  local copies, waits for them, and re-layouts  20 us (6%)
  Pallas kernels  12.3 us (4%)
  other arithmetic  6.96 us (2%)
  matrix products  6.34 us (2%)
    ppermute x21, starting transfers between devices, shifted(): lax.ppermute(array, 'hidden', [(i, (i + step) % devices) for i in range(d...  67.9 us
    all_to_all x2, waiting for transfers between devices, sent(): return lax.all_to_all(tiles, axes, split_axis=0, concat_axis=0, tiled=True)  64.8 us
    all_to_all x2, starting transfers between devices, sent(): return lax.all_to_all(tiles, axes, split_axis=0, concat_axis=0, tiled=True)  50.9 us
    all_to_all x1, blocking collectives, sent(): return lax.all_to_all(tiles, axes, split_axis=0, concat_axis=0, tiled=True)  48.7 us
    ppermute x21, waiting for transfers between devices, shifted(): lax.ppermute(array, 'hidden', [(i, (i + step) % devices) for i in range(d...  32.8 us
    unnamed x68, local copies, waits for them, and re-layouts  16 us
    pallas_call x2, Pallas kernels, add_blocks(): pl.pallas_call(body, out_shape=done if finish else shapes, in_specs=[pl.B...  9.63 us
  transfers between devices with their start and end apart: 23, of which 6 were waited for; matrix products, arithmetic and copies ran while one was open for 3% of the time, Pallas kernels for 3%

profile of v2, /device:TPU:65, one launch (start us, length us, event | category | flops | bytes accessed | tf_op | source)
XLA Modules:
  0.0 311.5 jit_solution(14164352373614903348)
XLA Ops:
  2.8 45.8 %all-to-all-start = ((bf16[32,24,512]{2,1,0:T(8,128)(2,1)}), bf16[32,24,512]{2,1,0:T(8,128)(2,1)}, u32[]{:S(2)}, u32[]{:S(2)}) async-start(bf16[32,24,512]{2,1,0:T(8,128)(2,1)} %bitcast.13), calls=%async_computation | async-start | bytes 1572864 | tf_op jit(solution)/shard_map/all_to_all | solution.py:29
  50.6 2.8 collective-permute-start.18
  53.4 4.4 %collective-permute-start.19 = (bf16[200,512]{1,0:T(8,128)(2,1)}, bf16[200,512]{1,0:T(8,128)(2,1)}, u32[]{:S(2)}, u32[]{:S(2)}) collective-permute-start(bf16[200,512]{1,0:T(8,128)(2,1)} %get-tuple-element.33), channel_id=1, source_target_pairs={{0,2},{1,3},{2,4},{3,5},{4,6},{5,7},{6,0},{7,1},{8,10},{9,11},{10,... | collective-permute-start | bytes 614408 | tf_op jit(solution)/shard_map/ppermute | solution.py:21
  57.8 35.4 %all-to-all-done = bf16[32,24,512]{2,1,0:T(8,128)(2,1)} async-done(((bf16[32,24,512]{2,1,0:T(8,128)(2,1)}), bf16[32,24,512]{2,1,0:T(8,128)(2,1)}, u32[]{:S(2)}, u32[]{:S(2)}) %all-to-all-start) | async-done | bytes 786464 | tf_op jit(solution)/shard_map/all_to_all | solution.py:29
  94.4 4.7 %collective-permute-start.13 = (bf16[384,512]{1,0:T(8,128)(2,1)S(1)}, bf16[384,512]{1,0:T(8,128)(2,1)S(1)}, u32[]{:S(2)}, u32[]{:S(2)}) collective-permute-start(bf16[384,512]{1,0:T(8,128)(2,1)S(1)} %bitcast.34), channel_id=1, source_target_pairs={{0,7},{1,0},{2,1},{3,2},{4,3},{5,4},{6,5},{7,6},{8,15},{9,8},{10,9... | collective-permute-start | bytes 1179656 | tf_op jit(solution)/shard_map/ppermute | solution.py:21
  102.1 5.6 %collective-permute-start.3 = (bf16[104,512]{1,0:T(8,128)(2,1)S(1)}, bf16[104,512]{1,0:T(8,128)(2,1)S(1)}, u32[]{:S(2)}, u32[]{:S(2)}) collective-permute-start(bf16[104,512]{1,0:T(8,128)(2,1)S(1)} %pad_maximum_fusion.7), channel_id=1, source_target_pairs={{0,4},{1,5},{2,6},{3,7},{4,0},{5,1},{6,2},{7,3},{8,12},{9,13},{10,... | collective-permute-start | bytes 319496 | tf_op jit(solution)/shard_map/ppermute | solution.py:21
  107.7 9.7 %collective-permute-done.3.refs_2_.refs_4_ = bf16[104,512]{1,0:T(8,128)(2,1)S(1)} collective-permute-done((bf16[104,512]{1,0:T(8,128)(2,1)S(1)}, bf16[104,512]{1,0:T(8,128)(2,1)S(1)}, u32[]{:S(2)}, u32[]{:S(2)}) %collective-permute-start.3) | collective-permute-done | bytes 106528 | tf_op jit(solution)/shard_map/ppermute | solution.py:21
  121.3 3.4 %collective-permute-start.7 = (bf16[384,512]{1,0:T(8,128)(2,1)S(1)}, bf16[384,512]{1,0:T(8,128)(2,1)S(1)}, u32[]{:S(2)}, u32[]{:S(2)}) collective-permute-start(bf16[384,512]{1,0:T(8,128)(2,1)S(1)} %bitcast.35), channel_id=1, source_target_pairs={{0,1},{1,2},{2,3},{3,4},{4,5},{5,6},{6,7},{7,0},{8,9},{9,10},{10,1... | collective-permute-start | bytes 1179656 | tf_op jit(solution)/shard_map/ppermute | solution.py:21
  124.8 3.1 %collective-permute-start.5 = (bf16[384,512]{1,0:T(8,128)(2,1)S(1)}, bf16[384,512]{1,0:T(8,128)(2,1)S(1)}, u32[]{:S(2)}, u32[]{:S(2)}) collective-permute-start(bf16[384,512]{1,0:T(8,128)(2,1)S(1)} %collective-permute-done.4.refs_7_), channel_id=1, source_target_pairs={{0,1},{1,2},{2,3},{3,4},{4,5},{5,6},{6,7},{7,0},{8,9},{9,10},{10,1... | collective-permute-start | bytes 1179656 | tf_op jit(solution)/shard_map/ppermute | solution.py:21
  128.6 3.4 %collective-permute-start.14 = (bf16[384,512]{1,0:T(8,128)(2,1)S(1)}, bf16[384,512]{1,0:T(8,128)(2,1)S(1)}, u32[]{:S(2)}, u32[]{:S(2)}) collective-permute-start(bf16[384,512]{1,0:T(8,128)(2,1)S(1)} %collective-permute-done.13.refs_10_), channel_id=1, source_target_pairs={{0,7},{1,0},{2,1},{3,2},{4,3},{5,4},{6,5},{7,6},{8,15},{9,8},{10,9... | collective-permute-start | bytes 1179656 | tf_op jit(solution)/shard_map/ppermute | solution.py:21
  136.2 5.3 %collective-permute-start.11 = (bf16[384,512]{1,0:T(8,128)(2,1)S(1)}, bf16[384,512]{1,0:T(8,128)(2,1)}, u32[]{:S(2)}, u32[]{:S(2)}) collective-permute-start(bf16[384,512]{1,0:T(8,128)(2,1)S(1)} %collective-permute-done.10.refs_9_), channel_id=1, source_target_pairs={{0,7},{1,0},{2,1},{3,2},{4,3},{5,4},{6,5},{7,6},{8,15},{9,8},{10,9... | collective-permute-start | bytes 1179656 | tf_op jit(solution)/shard_map/ppermute | solution.py:21
  147.7 4.6 %collective-permute-start.15 = (bf16[384,512]{1,0:T(8,128)(2,1)S(1)}, bf16[384,512]{1,0:T(8,128)(2,1)}, u32[]{:S(2)}, u32[]{:S(2)}) collective-permute-start(bf16[384,512]{1,0:T(8,128)(2,1)S(1)} %collective-permute-done.14.refs_14_), channel_id=1, source_target_pairs={{0,7},{1,0},{2,1},{3,2},{4,3},{5,4},{6,5},{7,6},{8,15},{9,8},{10,9... | collective-permute-start | bytes 1179656 | tf_op jit(solution)/shard_map/ppermute | solution.py:21
  157.4 14.4 %collective-permute-done.refs_0_.refs_3_ = bf16[200,512]{1,0:T(8,128)(2,1)S(1)} collective-permute-done((bf16[200,512]{1,0:T(8,128)(2,1)}, bf16[200,512]{1,0:T(8,128)(2,1)S(1)}, u32[]{:S(2)}, u32[]{:S(2)}) %collective-permute-start) | collective-permute-done | bytes 204832 | tf_op jit(solution)/shard_map/ppermute | solution.py:21
  172.6 4.5 %collective-permute-start.2 = (bf16[296,512]{1,0:T(8,128)(2,1)}, bf16[296,512]{1,0:T(8,128)(2,1)}, u32[]{:S(2)}, u32[]{:S(2)}) collective-permute-start(bf16[296,512]{1,0:T(8,128)(2,1)} %fusion.11), channel_id=1, source_target_pairs={{0,5},{1,6},{2,7},{3,0},{4,1},{5,2},{6,3},{7,4},{8,13},{9,14},{10,... | collective-permute-start | bytes 909320 | tf_op jit(solution)/shard_map/ppermute | solution.py:21
  179.1 3.4 %collective-permute-start.9 = (bf16[384,512]{1,0:T(8,128)(2,1)}, bf16[384,512]{1,0:T(8,128)(2,1)}, u32[]{:S(2)}, u32[]{:S(2)}) collective-permute-start(bf16[384,512]{1,0:T(8,128)(2,1)} %collective-permute-done.8.refs_12_), channel_id=1, source_target_pairs={{0,1},{1,2},{2,3},{3,4},{4,5},{5,6},{6,7},{7,0},{8,9},{9,10},{10,1... | collective-permute-start | bytes 1179656 | tf_op jit(solution)/shard_map/ppermute | solution.py:21
  182.5 5.2 %collective-permute-start.16 = (bf16[384,512]{1,0:T(8,128)(2,1)}, bf16[384,512]{1,0:T(8,128)(2,1)}, u32[]{:S(2)}, u32[]{:S(2)}) collective-permute-start(bf16[384,512]{1,0:T(8,128)(2,1)} %collective-permute-done.6.refs_3_), channel_id=1, source_target_pairs={{0,1},{1,2},{2,3},{3,4},{4,5},{5,6},{6,7},{7,0},{8,9},{9,10},{10,1... | collective-permute-start | bytes 1179656 | tf_op jit(solution)/shard_map/ppermute | solution.py:21
  202.4 5.7 %shard_map.82 = (f32[384,768]{1,0:T(8,128)S(1)}, f32[768,128]{1,0:T(8,128)S(1)}) custom-call(s32[8]{0:T(128)S(1)} %stack.35.turn, bf16[2,96,4096]{2,1,0:T(8,128)(2,1)S(1)} %copy-done.1, bf16[2,96,4096]{2,1,0:T(8,128)(2,1)S(1)} %copy-done.2, bf16[200,512]{1,0:T(8,128)(2,1)S(1)} %get-tuple-element.31.refs_0_, ...), custom_call_target="tpu_custom_call" | custom-call | flops 1509949440 | tf_op jit(solution)/shard_map/pallas_call | solution.py:151
  208.1 7.4 %collective-permute-done.17.refs_8_ = bf16[384,512]{1,0:T(8,128)(2,1)} collective-permute-done((bf16[384,512]{1,0:T(8,128)(2,1)}, bf16[384,512]{1,0:T(8,128)(2,1)}, u32[]{:S(2)}, u32[]{:S(2)}) %collective-permute-start.17) | collective-permute-done | bytes 393248 | tf_op jit(solution)/shard_map/ppermute | solution.py:21
  215.5 3.9 %shard_map.83 = bf16[8,96,768]{2,1,0:T(8,128)(2,1)S(1)} custom-call(s32[8]{0:T(128)S(1)} %stack.35.turn, bf16[2,96,4096]{2,1,0:T(8,128)(2,1)S(1)} %copy-done.1, bf16[2,96,4096]{2,1,0:T(8,128)(2,1)S(1)} %copy-done.2, bf16[200,512]{1,0:T(8,128)(2,1)S(1)} %copy-done.15, bf16[296,512]{1,0:T(8,128)(2,1)} %collective-permute-done.2.refs_1_.refs_5_, ...), custom_call_target="tpu_custom_call" | custom-call | flops 905969664 | tf_op jit(solution)/shard_map/pallas_call | solution.py:151
  220.5 5.1 %all-to-all-start.1 = ((bf16[8,96,768]{2,1,0:T(8,128)(2,1)}), bf16[8,96,768]{2,1,0:T(8,128)(2,1)}, u32[]{:S(2)}, u32[]{:S(2)}) async-start(bf16[8,96,768]{2,1,0:T(8,128)(2,1)} %copy-done.3), calls=%async_computation.1 | async-start | bytes 2359296 | tf_op jit(solution)/shard_map/all_to_all | solution.py:29
  225.6 2.7 shard_map.84
  228.3 29.4 %all-to-all-done.1 = bf16[8,96,768]{2,1,0:T(8,128)(2,1)} async-done(((bf16[8,96,768]{2,1,0:T(8,128)(2,1)}), bf16[8,96,768]{2,1,0:T(8,128)(2,1)}, u32[]{:S(2)}, u32[]{:S(2)}) %all-to-all-start.1) | async-done | bytes 1179680 | tf_op jit(solution)/shard_map/all_to_all | solution.py:29
  259.8 2.1 fusion
  261.9 48.7 %all_to_all.15 = bf16[32,24,512]{2,1,0:T(8,128)(2,1)S(1)} all-to-all(bf16[32,24,512]{2,1,0:T(8,128)(2,1)S(1)} %bitcast.41), channel_id=1, replica_groups=mesh['groups'=2,'expert_0'=16,'expert_1'=2,'hidden'=8] {'expert_0','expe..., dimensions={0} | all-to-all | bytes 1572864 | tf_op jit(solution)/shard_map/all_to_all | solution.py:29
  (115 shorter events, 50.0 us)
Async XLA Ops:
  2.8 90.5 %all-to-all-start = ((bf16[32,24,512]{2,1,0:T(8,128)(2,1)}), bf16[32,24,512]{2,1,0:T(8,128)(2,1)}, u32[]{:S(2)}, u32[]{:S(2)}) async-start(bf16[32,24,512]{2,1,0:T(8,128)(2,1)} %bitcast.13), calls=%async_computation | async-start | bytes 1572864 | tf_op jit(solution)/shard_map/all_to_all | solution.py:29
  50.6 68.7 %collective-permute-start.18 = (bf16[200,512]{1,0:T(8,128)(2,1)}, bf16[200,512]{1,0:T(8,128)(2,1)}, u32[]{:S(2)}, u32[]{:S(2)}) collective-permute-start(bf16[200,512]{1,0:T(8,128)(2,1)} %get-tuple-element.32), channel_id=1, source_target_pairs={{0,1},{1,2},{2,3},{3,4},{4,5},{5,6},{6,7},{7,0},{8,9},{9,10},{10,1... | collective-permute-start | bytes 614408 | tf_op jit(solution)/shard_map/ppermute | solution.py:21
  53.4 67.9 %collective-permute-start.19 = (bf16[200,512]{1,0:T(8,128)(2,1)}, bf16[200,512]{1,0:T(8,128)(2,1)}, u32[]{:S(2)}, u32[]{:S(2)}) collective-permute-start(bf16[200,512]{1,0:T(8,128)(2,1)} %get-tuple-element.33), channel_id=1, source_target_pairs={{0,2},{1,3},{2,4},{3,5},{4,6},{5,7},{6,0},{7,1},{8,10},{9,11},{10,... | collective-permute-start | bytes 614408 | tf_op jit(solution)/shard_map/ppermute | solution.py:21
  57.8 134.7 %copy-start.1 = (bf16[2,96,4096]{2,1,0:T(8,128)(2,1)S(1)}, bf16[2,96,4096]{2,1,0:T(8,128)(2,1)}, u32[]{:S(2)}) copy-start(bf16[2,96,4096]{2,1,0:T(8,128)(2,1)} %gate.3) | copy-start | bytes 4718596
  94.4 34.2 %collective-permute-start.13 = (bf16[384,512]{1,0:T(8,128)(2,1)S(1)}, bf16[384,512]{1,0:T(8,128)(2,1)S(1)}, u32[]{:S(2)}, u32[]{:S(2)}) collective-permute-start(bf16[384,512]{1,0:T(8,128)(2,1)S(1)} %bitcast.34), channel_id=1, source_target_pairs={{0,7},{1,0},{2,1},{3,2},{4,3},{5,4},{6,5},{7,6},{8,15},{9,8},{10,9... | collective-permute-start | bytes 1179656 | tf_op jit(solution)/shard_map/ppermute | solution.py:21
  99.1 25.6 %collective-permute-start.4 = (bf16[384,512]{1,0:T(8,128)(2,1)S(1)}, bf16[384,512]{1,0:T(8,128)(2,1)S(1)}, u32[]{:S(2)}, u32[]{:S(2)}) collective-permute-start(bf16[384,512]{1,0:T(8,128)(2,1)S(1)} %bitcast.37), channel_id=1, source_target_pairs={{0,1},{1,2},{2,3},{3,4},{4,5},{5,6},{6,7},{7,0},{8,9},{9,10},{10,1... | collective-permute-start | bytes 1179656 | tf_op jit(solution)/shard_map/ppermute | solution.py:21
  102.1 15.3 %collective-permute-start.3 = (bf16[104,512]{1,0:T(8,128)(2,1)S(1)}, bf16[104,512]{1,0:T(8,128)(2,1)S(1)}, u32[]{:S(2)}, u32[]{:S(2)}) collective-permute-start(bf16[104,512]{1,0:T(8,128)(2,1)S(1)} %pad_maximum_fusion.7), channel_id=1, source_target_pairs={{0,4},{1,5},{2,6},{3,7},{4,0},{5,1},{6,2},{7,3},{8,12},{9,13},{10,... | collective-permute-start | bytes 319496 | tf_op jit(solution)/shard_map/ppermute | solution.py:21
  117.4 15.6 %collective-permute-start.20 = (bf16[200,512]{1,0:T(8,128)(2,1)}, bf16[200,512]{1,0:T(8,128)(2,1)S(1)}, u32[]{:S(2)}, u32[]{:S(2)}) collective-permute-start(bf16[200,512]{1,0:T(8,128)(2,1)} %get-tuple-element.30), channel_id=1, source_target_pairs={{0,6},{1,7},{2,0},{3,1},{4,2},{5,3},{6,4},{7,5},{8,14},{9,15},{10,... | collective-permute-start | bytes 614408 | tf_op jit(solution)/shard_map/ppermute | solution.py:21
  119.4 16.8 %collective-permute-start.10 = (bf16[384,512]{1,0:T(8,128)(2,1)S(1)}, bf16[384,512]{1,0:T(8,128)(2,1)S(1)}, u32[]{:S(2)}, u32[]{:S(2)}) collective-permute-start(bf16[384,512]{1,0:T(8,128)(2,1)S(1)} %bitcast.38), channel_id=1, source_target_pairs={{0,7},{1,0},{2,1},{3,2},{4,3},{5,4},{6,5},{7,6},{8,15},{9,8},{10,9... | collective-permute-start | bytes 1179656 | tf_op jit(solution)/shard_map/ppermute | solution.py:21
  121.3 21.0 %collective-permute-start.7 = (bf16[384,512]{1,0:T(8,128)(2,1)S(1)}, bf16[384,512]{1,0:T(8,128)(2,1)S(1)}, u32[]{:S(2)}, u32[]{:S(2)}) collective-permute-start(bf16[384,512]{1,0:T(8,128)(2,1)S(1)} %bitcast.35), channel_id=1, source_target_pairs={{0,1},{1,2},{2,3},{3,4},{4,5},{5,6},{6,7},{7,0},{8,9},{9,10},{10,1... | collective-permute-start | bytes 1179656 | tf_op jit(solution)/shard_map/ppermute | solution.py:21
  124.8 20.3 %collective-permute-start.5 = (bf16[384,512]{1,0:T(8,128)(2,1)S(1)}, bf16[384,512]{1,0:T(8,128)(2,1)S(1)}, u32[]{:S(2)}, u32[]{:S(2)}) collective-permute-start(bf16[384,512]{1,0:T(8,128)(2,1)S(1)} %collective-permute-done.4.refs_7_), channel_id=1, source_target_pairs={{0,1},{1,2},{2,3},{3,4},{4,5},{5,6},{6,7},{7,0},{8,9},{9,10},{10,1... | collective-permute-start | bytes 1179656 | tf_op jit(solution)/shard_map/ppermute | solution.py:21
  128.6 19.1 %collective-permute-start.14 = (bf16[384,512]{1,0:T(8,128)(2,1)S(1)}, bf16[384,512]{1,0:T(8,128)(2,1)S(1)}, u32[]{:S(2)}, u32[]{:S(2)}) collective-permute-start(bf16[384,512]{1,0:T(8,128)(2,1)S(1)} %collective-permute-done.13.refs_10_), channel_id=1, source_target_pairs={{0,7},{1,0},{2,1},{3,2},{4,3},{5,4},{6,5},{7,6},{8,15},{9,8},{10,9... | collective-permute-start | bytes 1179656 | tf_op jit(solution)/shard_map/ppermute | solution.py:21
  133.0 20.0 %collective-permute-start.1 = (bf16[296,512]{1,0:T(8,128)(2,1)S(1)}, bf16[296,512]{1,0:T(8,128)(2,1)S(1)}, u32[]{:S(2)}, u32[]{:S(2)}) collective-permute-start(bf16[296,512]{1,0:T(8,128)(2,1)S(1)} %fusion.12), channel_id=1, source_target_pairs={{0,7},{1,0},{2,1},{3,2},{4,3},{5,4},{6,5},{7,6},{8,15},{9,8},{10,9... | collective-permute-start | bytes 909320 | tf_op jit(solution)/shard_map/ppermute | solution.py:21
  136.2 40.9 %collective-permute-start.11 = (bf16[384,512]{1,0:T(8,128)(2,1)S(1)}, bf16[384,512]{1,0:T(8,128)(2,1)}, u32[]{:S(2)}, u32[]{:S(2)}) collective-permute-start(bf16[384,512]{1,0:T(8,128)(2,1)S(1)} %collective-permute-done.10.refs_9_), channel_id=1, source_target_pairs={{0,7},{1,0},{2,1},{3,2},{4,3},{5,4},{6,5},{7,6},{8,15},{9,8},{10,9... | collective-permute-start | bytes 1179656 | tf_op jit(solution)/shard_map/ppermute | solution.py:21
  142.3 36.8 %collective-permute-start.8 = (bf16[384,512]{1,0:T(8,128)(2,1)S(1)}, bf16[384,512]{1,0:T(8,128)(2,1)}, u32[]{:S(2)}, u32[]{:S(2)}) collective-permute-start(bf16[384,512]{1,0:T(8,128)(2,1)S(1)} %collective-permute-done.7.refs_8_), channel_id=1, source_target_pairs={{0,1},{1,2},{2,3},{3,4},{4,5},{5,6},{6,7},{7,0},{8,9},{9,10},{10,1... | collective-permute-start | bytes 1179656 | tf_op jit(solution)/shard_map/ppermute | solution.py:21
  145.0 37.5 %collective-permute-start.6 = (bf16[384,512]{1,0:T(8,128)(2,1)S(1)}, bf16[384,512]{1,0:T(8,128)(2,1)}, u32[]{:S(2)}, u32[]{:S(2)}) collective-permute-start(bf16[384,512]{1,0:T(8,128)(2,1)S(1)} %collective-permute-done.5.refs_11_), channel_id=1, source_target_pairs={{0,1},{1,2},{2,3},{3,4},{4,5},{5,6},{6,7},{7,0},{8,9},{9,10},{10,1... | collective-permute-start | bytes 1179656 | tf_op jit(solution)/shard_map/ppermute | solution.py:21
  147.7 40.0 %collective-permute-start.15 = (bf16[384,512]{1,0:T(8,128)(2,1)S(1)}, bf16[384,512]{1,0:T(8,128)(2,1)}, u32[]{:S(2)}, u32[]{:S(2)}) collective-permute-start(bf16[384,512]{1,0:T(8,128)(2,1)S(1)} %collective-permute-done.14.refs_14_), channel_id=1, source_target_pairs={{0,7},{1,0},{2,1},{3,2},{4,3},{5,4},{6,5},{7,6},{8,15},{9,8},{10,9... | collective-permute-start | bytes 1179656 | tf_op jit(solution)/shard_map/ppermute | solution.py:21
  153.1 18.8 %collective-permute-start = (bf16[200,512]{1,0:T(8,128)(2,1)}, bf16[200,512]{1,0:T(8,128)(2,1)S(1)}, u32[]{:S(2)}, u32[]{:S(2)}) collective-permute-start(bf16[200,512]{1,0:T(8,128)(2,1)} %get-tuple-element.34), channel_id=1, source_target_pairs={{0,3},{1,4},{2,5},{3,6},{4,7},{5,0},{6,1},{7,2},{8,11},{9,12},{10,... | collective-permute-start | bytes 614408 | tf_op jit(solution)/shard_map/ppermute | solution.py:21
  172.6 35.5 %collective-permute-start.2 = (bf16[296,512]{1,0:T(8,128)(2,1)}, bf16[296,512]{1,0:T(8,128)(2,1)}, u32[]{:S(2)}, u32[]{:S(2)}) collective-permute-start(bf16[296,512]{1,0:T(8,128)(2,1)} %fusion.11), channel_id=1, source_target_pairs={{0,5},{1,6},{2,7},{3,0},{4,1},{5,2},{6,3},{7,4},{8,13},{9,14},{10,... | collective-permute-start | bytes 909320 | tf_op jit(solution)/shard_map/ppermute | solution.py:21
  177.1 31.0 %collective-permute-start.12 = (bf16[384,512]{1,0:T(8,128)(2,1)}, bf16[384,512]{1,0:T(8,128)(2,1)}, u32[]{:S(2)}, u32[]{:S(2)}) collective-permute-start(bf16[384,512]{1,0:T(8,128)(2,1)} %collective-permute-done.11.refs_13_), channel_id=1, source_target_pairs={{0,7},{1,0},{2,1},{3,2},{4,3},{5,4},{6,5},{7,6},{8,15},{9,8},{10,9... | collective-permute-start | bytes 1179656 | tf_op jit(solution)/shard_map/ppermute | solution.py:21
  179.1 29.0 %collective-permute-start.9 = (bf16[384,512]{1,0:T(8,128)(2,1)}, bf16[384,512]{1,0:T(8,128)(2,1)}, u32[]{:S(2)}, u32[]{:S(2)}) collective-permute-start(bf16[384,512]{1,0:T(8,128)(2,1)} %collective-permute-done.8.refs_12_), channel_id=1, source_target_pairs={{0,1},{1,2},{2,3},{3,4},{4,5},{5,6},{6,7},{7,0},{8,9},{9,10},{10,1... | collective-permute-start | bytes 1179656 | tf_op jit(solution)/shard_map/ppermute | solution.py:21
  182.5 25.6 %collective-permute-start.16 = (bf16[384,512]{1,0:T(8,128)(2,1)}, bf16[384,512]{1,0:T(8,128)(2,1)}, u32[]{:S(2)}, u32[]{:S(2)}) collective-permute-start(bf16[384,512]{1,0:T(8,128)(2,1)} %collective-permute-done.6.refs_3_), channel_id=1, source_target_pairs={{0,1},{1,2},{2,3},{3,4},{4,5},{5,6},{6,7},{7,0},{8,9},{9,10},{10,1... | collective-permute-start | bytes 1179656 | tf_op jit(solution)/shard_map/ppermute | solution.py:21
  187.7 27.8 %collective-permute-start.17 = (bf16[384,512]{1,0:T(8,128)(2,1)}, bf16[384,512]{1,0:T(8,128)(2,1)}, u32[]{:S(2)}, u32[]{:S(2)}) collective-permute-start(bf16[384,512]{1,0:T(8,128)(2,1)} %collective-permute-done.15.refs_6_), channel_id=1, source_target_pairs={{0,7},{1,0},{2,1},{3,2},{4,3},{5,4},{6,5},{7,6},{8,15},{9,8},{10,9... | collective-permute-start | bytes 1179656 | tf_op jit(solution)/shard_map/ppermute | solution.py:21
  220.5 37.2 %all-to-all-start.1 = ((bf16[8,96,768]{2,1,0:T(8,128)(2,1)}), bf16[8,96,768]{2,1,0:T(8,128)(2,1)}, u32[]{:S(2)}, u32[]{:S(2)}) async-start(bf16[8,96,768]{2,1,0:T(8,128)(2,1)} %copy-done.3), calls=%async_computation.1 | async-start | bytes 2359296 | tf_op jit(solution)/shard_map/all_to_all | solution.py:29
  (33 other events, 601.5 us)
